TPU v7x, 128 devices: a 2x2x16 block of a 8x8x16 slice. The times are simulated.
128 devices in a mesh: groups: 4 (over x, y), tm: 16 (over z), rows: 2 (over core).
Axes of the slice: x: 2, y: 2, z: 16, core: 2. Of those that a mesh axis runs over, the one named last changes fastest.
The devices are a block of a 8x8x16 slice.
Arguments:
- iterate: float32 [128, 512, 512], P(('groups', 'tm'), 'rows'), parts along dimension 0, may hold values from -6 to 6
- forcing: float32 [128, 512, 512], P(('groups', 'tm'), 'rows'), parts along dimension 0, may hold values from -18 to 18
- initial_state: float32 [2048, 512], P(('groups', 'rows')), parts along dimension 0, may hold values from -6 to 6
- diffusivity: float32 [2048, 512], P(('groups', 'rows')), parts along dimension 0, may hold values from 0.5 to 4
Outputs:
- updated: float32 [128, 512, 512], P(('groups', 'tm'), 'rows'), parts along dimension 0
- residual_rms: float32 [128], P(('groups', 'tm')), parts along dimension 0
There are 4 independent parts, one for each index of `groups`. A program takes and returns all parts, laid end to end along the dimension named above; each array names one. Nothing has to cross between parts.
All inputs are finite; a program needn't handle non-finite values.
Results may differ from a plain program's by a relative error of at most 0.0003.
Values sent between devices are 32-bit elements; how exact they have to be, the bound alone decides.
A program may use at most 64 MiB of HBM per device.

v0:
```python
import jax
import jax.numpy as jnp
from jax import lax
from jax.sharding import PartitionSpec as P

CG_ITERS = 3


circulant_alpha = 0.05
time_step = 0.5
rms_eps = 1e-06


def extended(block, sides, width):
    for axis, dim in sides:
        count = lax.axis_size(axis)
        forward = [(i, i + 1) for i in range(count - 1)]
        backward = [(target, source) for source, target in forward]
        low = lax.ppermute(
            lax.slice_in_dim(block, block.shape[dim] - width, None, axis=dim), axis, forward
        )
        high = lax.ppermute(lax.slice_in_dim(block, 0, width, axis=dim), axis, backward)
        block = jnp.concatenate([low, block, high], axis=dim)
    return block


def from_behind(value, axis, steps):
    count = lax.axis_size(axis)
    initial, last = (max(0, -steps), min(count, count - steps))
    return lax.ppermute(value, axis, [(source, source + steps) for source in range(initial, last)])


def over_pieces(value, axis):
    tiles = lax.all_gather(value, axis)
    return tiles.sum(axis=0)


def split_up(value, dim, count):
    before, after = (value.shape[:dim], value.shape[dim + 1 :])
    return jnp.moveaxis(value.reshape(*before, count, -1, *after), dim, 0)


def joined_along(tiles, dim):
    tiles = jnp.moveaxis(tiles, 0, dim)
    dims = tiles.shape
    return tiles.reshape(*dims[:dim], dims[dim] * dims[dim + 1], *dims[dim + 2 :])


def exchange_both(value, axis, axes, splits, concats):
    sizes = [lax.axis_size(a) for a in axes]
    tiles = split_up(value, splits[0], sizes[0])
    tiles = jnp.moveaxis(split_up(tiles, splits[1] + 1, sizes[1]), 0, 1)
    inside = tiles.shape[2:]
    tiles = tiles.reshape(-1, *inside)
    tiles = lax.all_to_all(tiles, axis, split_axis=0, concat_axis=0, tiled=True)
    tiles = joined_along(tiles.reshape(*sizes, *inside), concats[0] + 1)
    return joined_along(tiles, concats[1])


def from_everyone(value, axis):
    count = lax.axis_size(axis)
    return lax.all_to_all(
        jnp.broadcast_to(value[None], (count, *value.shape)), axis, 0, 0, tiled=True
    )


def collect(value, axis, dim):
    tiles = from_everyone(value, axis)
    return joined_along(tiles, dim)


def phase_table(first_index, second_index, length):
    product = first_index[:, None] * second_index[None, :] % length
    return 2.0 * jnp.pi / length * product.astype(jnp.float32)


def faces_from(padded_rows):
    centre = padded_rows[1:-1]
    columns = jnp.pad(centre, ((0, 0), (1, 1)), mode="edge")
    north_face = 0.5 * (centre + padded_rows[:-2])
    south_face = 0.5 * (centre + padded_rows[2:])
    west_face = 0.5 * (centre + columns[:, :-2])
    east_face = 0.5 * (centre + columns[:, 2:])
    return (north_face, south_face, west_face, east_face)


def apply_faces(padded_rows, weights):
    north_face, south_face, west_face, east_face = weights
    centre = padded_rows[..., 1:-1, :]
    lead_pad = [(0, 0)] * (centre.ndim - 1)
    columns = jnp.pad(centre, lead_pad + [(1, 1)])
    return (
        (north_face + south_face + west_face + east_face) * centre
        - north_face * padded_rows[..., :-2, :]
        - south_face * padded_rows[..., 2:, :]
        - west_face * columns[..., :-2]
        - east_face * columns[..., 2:]
    )


def high_dot(first_mat, second_mat):
    return jnp.dot(
        first_mat, second_mat, precision=lax.Precision.HIGHEST, preferred_element_type=jnp.float32
    )


def shards(iterate, forcing, initial_state, diffusivity):
    steps_dev, rows_dev, columns_dev = iterate.shape
    time_devices = lax.axis_size("tm")
    row_devices = lax.axis_size("rows")
    time_rank = lax.axis_index("tm")
    row_rank = lax.axis_index("rows")
    length = steps_dev * time_devices
    cell_count = rows_dev * row_devices * columns_dev
    rimmed = extended(diffusivity, (("rows", 0),), 1)
    top_row = jnp.where(row_rank == 0, diffusivity[:1], rimmed[:1])
    bottom_row = jnp.where(row_rank == row_devices - 1, diffusivity[-1:], rimmed[-1:])
    rimmed = jnp.concatenate([top_row, rimmed[1:-1], bottom_row], axis=0)
    local_faces = faces_from(rimmed)
    arriving = from_behind(iterate[-1], "tm", 1)
    first_previous = jnp.where(time_rank == 0, initial_state, arriving)
    previous = jnp.concatenate([first_previous[None], iterate[:-1]], axis=0)
    iterate_rim = extended(iterate, (("rows", 1),), 1)
    residual = (
        time_step * forcing + previous - iterate - time_step * apply_faces(iterate_rim, local_faces)
    )
    squares = over_pieces(jnp.sum(residual * residual, axis=(1, 2)), "rows")
    residual_rms = jnp.sqrt(squares / cell_count + rms_eps)
    step_index = time_rank * steps_dev + jnp.arange(steps_dev, dtype=jnp.int32)
    log_alpha = jnp.log(jnp.float32(circulant_alpha))
    growth = jnp.exp(log_alpha * step_index.astype(jnp.float32) / length)
    scaled = residual * growth[:, None, None]
    by_cells = lax.all_to_all(scaled, "tm", split_axis=1, concat_axis=0, tiled=True)
    slab_rows = by_cells.shape[1]
    all_index = jnp.arange(length, dtype=jnp.int32)
    angles = phase_table(all_index, all_index, length)
    flat_cells = by_cells.reshape(length, slab_rows * columns_dev)
    spectrum_real = high_dot(jnp.cos(angles), flat_cells)
    spectrum_imag = high_dot(-jnp.sin(angles), flat_cells)
    spectrum = jnp.stack([spectrum_real, spectrum_imag]).reshape(2, length, slab_rows, columns_dev)
    per_device = steps_dev // row_devices
    by_freq = exchange_both(spectrum, ("tm", "rows"), ("tm", "rows"), (1, 1), (2, 2))
    freq_index = (time_rank * row_devices + row_rank) * per_device + jnp.arange(
        per_device, dtype=jnp.int32
    )
    whole_diff = collect(diffusivity, "rows", 0)
    solve_faces = faces_from(jnp.pad(whole_diff, ((1, 1), (0, 0)), mode="edge"))

    def rim_rows(values):
        lead_pad = [(0, 0)] * (values.ndim - 2)
        return jnp.pad(values, lead_pad + [(1, 1), (0, 0)])

    root_alpha = jnp.exp(log_alpha / length)
    freq_angle = 2.0 * jnp.pi / length * freq_index.astype(jnp.float32)
    real_shift = (1.0 - root_alpha * jnp.cos(freq_angle))[:, None, None]
    imag_shift = (root_alpha * jnp.sin(freq_angle))[:, None, None]

    def operate(values, orientation):
        spread = time_step * apply_faces(rim_rows(values), solve_faces)
        swapped = jnp.stack([-values[1], values[0]])
        return real_shift * values + orientation * imag_shift * swapped + spread

    def freq_norm(values):
        return jnp.sum(values * values, axis=(0, 2, 3))

    def expand(values):
        return values[None, :, None, None]

    solution = jnp.zeros_like(by_freq)
    normal = operate(by_freq, -1.0)
    gamma_now = freq_norm(normal)
    search = normal
    remain = by_freq
    for iteration in range(CG_ITERS):
        image_now = operate(search, 1.0)
        step_rate = gamma_now / freq_norm(image_now)
        solution = solution + expand(step_rate) * search
        if iteration + 1 < CG_ITERS:
            remain = remain - expand(step_rate) * image_now
            normal = operate(remain, -1.0)
            gamma_next = freq_norm(normal)
            search = normal + expand(gamma_next / gamma_now) * search
            gamma_now = gamma_next
    blocks = solution.reshape(2, per_device, row_devices, rows_dev, columns_dev)
    back_cells = exchange_both(blocks, ("tm", "rows"), ("tm", "rows"), (3, 2), (1, 1))
    back_cells = back_cells.reshape(2, length, slab_rows, columns_dev)
    outer_block = all_index // (time_devices * per_device)
    middle = all_index // per_device % time_devices
    inner_index = all_index % per_device
    position_freq = (middle * row_devices + outer_block) * per_device + inner_index
    inverse_angles = phase_table(all_index, position_freq, length)
    flat_real = back_cells[0].reshape(length, slab_rows * columns_dev)
    flat_imag = back_cells[1].reshape(length, slab_rows * columns_dev)
    correction = high_dot(jnp.cos(inverse_angles) / length, flat_real) - high_dot(
        jnp.sin(inverse_angles) / length, flat_imag
    )
    correction = correction.reshape(length, slab_rows, columns_dev)
    own_steps = lax.all_to_all(correction, "tm", split_axis=0, concat_axis=1, tiled=True)
    updated = iterate + own_steps / growth[:, None, None]
    return (updated, residual_rms)


def solution(mesh):
    placed = (
        P(("groups", "tm"), "rows", None),
        P(("groups", "tm"), "rows", None),
        P(("groups", "rows"), None),
        P(("groups", "rows"), None),
    )
    return jax.shard_map(
        shards,
        mesh=mesh,
        in_specs=placed,
        out_specs=(P(("groups", "tm"), "rows", None), P(("groups", "tm"))),
        check_vma=False,
    )
```

profile of v0, /device:TPU:69, one launch (start us, length us, event | category | flops | bytes accessed | tf_op | source)
XLA Modules:
  0.0 436.4 jit_solution(5874704254902399163)
XLA Ops:
  0.6 0.8 fusion.141
  1.4 11.8 %collective-permute-start.2 = (f32[1,512]{1,0:T(1,128)S(1)}, f32[1,512]{1,0:T(1,128)S(1)}, u32[]{:S(2)}, u32[]{:S(2)}) collective-permute-start(f32[1,512]{1,0:T(1,128)S(1)} %get-tuple-element.52), channel_id=1, source_target_pairs={{1,0},{3,2},{5,4},{7,6},{9,8},{11,10},{13,12},{15,14},{17,16},{19,... | collective-permute-start | bytes 6152 | tf_op jit(solution)/shard_map/ppermute | solution.py:22
  13.3 1.3 collective-permute-start.1
  14.6 0.8 fusion.137
  15.4 1.3 collective-permute-start.3
  16.7 3.1 collective-permute-start.4
  19.8 1.3 slice_bitcast_fusion
  21.0 1.5 collective-permute-start
  22.7 0.4 add_add_fusion.1
  23.2 10.6 %collective-permute-done = f32[256,512]{1,0:T(8,128)S(1)} collective-permute-done((f32[256,512]{1,0:T(8,128)S(1)}, f32[256,512]{1,0:T(8,128)S(1)}, u32[]{:S(2)}, u32[]{:S(2)}) %collective-permute-start) | collective-permute-done | bytes 524320 | tf_op jit(solution)/shard_map/ppermute | solution.py:30
  33.9 1.1 multiply_reduce_fusion.5
  35.2 1.8 copy.58
  37.0 12.4 %all-to-all-start = ((f32[2,256,512]{2,0,1:T(2,128)}), f32[2,256,512]{2,0,1:T(2,128)S(1)}, u32[]{:S(2)}, u32[]{:S(2)}) async-start(f32[2,256,512]{2,0,1:T(2,128)} %copy.58), calls=%async_computation | async-start | bytes 2097152 | tf_op jit(solution)/shard_map/all_to_all | solution.py:133
  49.4 45.3 %all-to-all-done = f32[2,256,512]{2,0,1:T(2,128)S(1)} async-done(((f32[2,256,512]{2,0,1:T(2,128)}), f32[2,256,512]{2,0,1:T(2,128)S(1)}, u32[]{:S(2)}, u32[]{:S(2)}) %all-to-all-start) | async-done | bytes 1048608 | tf_op jit(solution)/shard_map/all_to_all | solution.py:133
  94.7 1.1 broadcast_in_dim.5
  95.8 9.0 %all-to-all-start.2 = ((f32[2,256,512]{2,1,0:T(8,128)}), f32[2,256,512]{2,1,0:T(8,128)S(1)}, u32[]{:S(2)}, u32[]{:S(2)}) async-start(f32[2,256,512]{2,1,0:T(8,128)} %broadcast_in_dim.5), calls=%async_computation.2 | async-start | bytes 2097152 | tf_op jit(solution)/shard_map/all_to_all | solution.py:62
  104.9 1.7 convolution_bitcast_fusion
  106.6 1.7 convolution_bitcast_fusion.1
  108.6 2.6 copy.62
  111.2 8.4 %all-to-all-start.1 = ((f32[32,2,1,16,512]{4,3,1,2,0:T(8,128)}), f32[32,2,1,16,512]{4,3,1,2,0:T(8,128)S(1)}, u32[]{:S(2)}, u32[]{:S(2)}) async-start(f32[32,2,1,16,512]{4,3,1,2,0:T(8,128)} %bitcast.19), calls=%async_computation.1 | async-start | bytes 4194304 | tf_op jit(solution)/shard_map/all_to_all | solution.py:55
  119.9 6.3 %add_add_fusion = (f32[512,512]{1,0:T(8,128)S(1)}, f32[512,512]{1,0:T(8,128)}, f32[512,512]{1,0:T(8,128)}, f32[512,512]{1,0:T(8,128)}, f32[512,512]{1,0:T(8,128)}) fusion(f32[512,512]{1,0:T(8,128)} %bitcast.118, f32[1,512]{1,0:T(1,128)S(1)} %get-tuple-element.47, f32[1,512]{1,0:T(1,128)S(1)} %get-tuple-element.46, f32[512,1]{1,0:T(8,128)S(1)} %get-tuple-element.45, ...), kind=kLoop, calls=%fused_computation.115 | loop fusion | flops 3932160 | bytes 6299648 | tf_op jit(solution)/shard_map/add | solution.py:93
  126.2 92.0 %all-to-all-done.1 = f32[32,2,1,16,512]{4,3,1,2,0:T(8,128)S(1)} async-done(((f32[32,2,1,16,512]{4,3,1,2,0:T(8,128)}), f32[32,2,1,16,512]{4,3,1,2,0:T(8,128)S(1)}, u32[]{:S(2)}, u32[]{:S(2)}) %all-to-all-start.1) | async-done | bytes 2097184 | tf_op jit(solution)/shard_map/all_to_all | solution.py:55
  218.9 1.1 copy-done.22
  219.9 0.7 copy-done.1
  220.6 0.3 copy-done.6
  220.9 0.3 copy-done.11
  221.2 0.3 copy-done.16
  221.5 3.0 multiply_reduce_fusion.4
  224.7 4.0 multiply_reduce_fusion.3
  230.0 2.7 multiply_subtract_fusion.1
  233.1 1.0 copy-done.21
  234.1 0.7 copy-done.2
  235.7 4.0 multiply_reduce_fusion.2
  241.0 2.1 multiply_add_fusion.2
  243.4 1.0 copy-done
  244.5 0.6 copy-done.3
  246.0 4.0 multiply_reduce_fusion.1
  251.4 2.7 multiply_subtract_fusion
  254.4 0.9 copy-done.4
  255.3 0.3 copy-done.9
  255.7 0.3 copy-done.14
  256.0 0.3 copy-done.19
  256.3 4.0 multiply_reduce_fusion
  261.6 2.7 multiply_add_fusion.1
  264.6 0.9 copy-done.5
  265.6 0.3 copy-done.10
  265.9 0.3 copy-done.15
  266.2 0.3 copy-done.20
  266.5 3.2 fusion.36
  271.0 3.0 multiply_add_fusion
  274.0 1.5 copy.68
  275.6 5.2 %all-to-all-start.3 = ((f32[32,2,1,1,16,512]{5,4,1,3,2,0:T(8,128)}), f32[32,2,1,1,16,512]{5,4,1,3,2,0:T(8,128)S(1)}, u32[]{:S(2)}, u32[]{:S(2)}) async-start(f32[32,2,1,1,16,512]{5,4,1,3,2,0:T(8,128)} %bitcast.114), calls=%async_computation.3 | async-start | bytes 4194304 | tf_op jit(solution)/shard_map/all_to_all | solution.py:55
  280.8 100.0 %all-to-all-done.3 = f32[32,2,1,1,16,512]{5,4,1,3,2,0:T(8,128)S(1)} async-done(((f32[32,2,1,1,16,512]{5,4,1,3,2,0:T(8,128)}), f32[32,2,1,1,16,512]{5,4,1,3,2,0:T(8,128)S(1)}, u32[]{:S(2)}, u32[]{:S(2)}) %all-to-all-start.3) | async-done | bytes 2097184 | tf_op jit(solution)/shard_map/all_to_all | solution.py:55
  381.3 0.6 copy.77
  382.0 0.6 copy.76
  382.6 1.1 fusion.89
  383.7 1.1 convolution_subtract_fusion
  384.8 1.6 copy.78
  386.3 4.2 all-to-all-start.4
  390.6 0.6 dynamic-slice
  392.1 3.7 all-reduce.13
  395.9 0.5 add_sqrt_fusion
  396.4 38.6 %all-to-all-done.4 = f32[32,16,512]{2,1,0:T(8,128)S(1)} async-done(((f32[32,16,512]{2,1,0:T(8,128)}), f32[32,16,512]{2,1,0:T(8,128)S(1)}, u32[]{:S(2)}, u32[]{:S(2)}) %all-to-all-start.4) | async-done | bytes 1048608 | tf_op jit(solution)/shard_map/all_to_all | solution.py:198
  435.1 1.3 fusion.63
  (74 shorter events, 5.7 us)
Async XLA Ops:
  0.6 21.9 %copy-start.26 = (f32[256,512]{1,0:T(8,128)S(1)}, f32[256,512]{1,0:T(8,128)}, u32[]{:S(2)}) copy-start(f32[256,512]{1,0:T(8,128)} %param.7) | copy-start | bytes 1572868
  1.4 21.2 %collective-permute-start.2 = (f32[1,512]{1,0:T(1,128)S(1)}, f32[1,512]{1,0:T(1,128)S(1)}, u32[]{:S(2)}, u32[]{:S(2)}) collective-permute-start(f32[1,512]{1,0:T(1,128)S(1)} %get-tuple-element.52), channel_id=1, source_target_pairs={{1,0},{3,2},{5,4},{7,6},{9,8},{11,10},{13,12},{15,14},{17,16},{19,... | collective-permute-start | bytes 6152 | tf_op jit(solution)/shard_map/ppermute | solution.py:22
  13.3 9.4 %collective-permute-start.1 = (f32[1,512]{1,0:T(1,128)S(1)}, f32[1,512]{1,0:T(1,128)S(1)}, u32[]{:S(2)}, u32[]{:S(2)}) collective-permute-start(f32[1,512]{1,0:T(1,128)S(1)} %get-tuple-element.53), channel_id=1, source_target_pairs={{0,1},{2,3},{4,5},{6,7},{8,9},{10,11},{12,13},{14,15},{16,17},{18,... | collective-permute-start | bytes 6152 | tf_op jit(solution)/shard_map/ppermute | solution.py:19
  15.4 18.5 %collective-permute-start.3 = (f32[2,1,512]{2,1,0:T(1,128)S(1)}, f32[2,1,512]{2,1,0:T(1,128)S(1)}, u32[]{:S(2)}, u32[]{:S(2)}) collective-permute-start(f32[2,1,512]{2,1,0:T(1,128)S(1)} %get-tuple-element.42), channel_id=1, source_target_pairs={{0,1},{2,3},{4,5},{6,7},{8,9},{10,11},{12,13},{14,15},{16,17},{18,... | collective-permute-start | bytes 12296 | tf_op jit(solution)/shard_map/ppermute | solution.py:19
  16.7 17.2 %collective-permute-start.4 = (f32[2,1,512]{2,1,0:T(1,128)S(1)}, f32[2,1,512]{2,1,0:T(1,128)S(1)}, u32[]{:S(2)}, u32[]{:S(2)}) collective-permute-start(f32[2,1,512]{2,1,0:T(1,128)S(1)} %get-tuple-element.43), channel_id=1, source_target_pairs={{1,0},{3,2},{5,4},{7,6},{9,8},{11,10},{13,12},{15,14},{17,16},{19,... | collective-permute-start | bytes 12296 | tf_op jit(solution)/shard_map/ppermute | solution.py:22
  21.0 12.7 %copy-start.28 = (f32[256,512]{1,0:T(8,128)S(1)}, f32[256,512]{1,0:T(8,128)}, u32[]{:S(2)}) copy-start(f32[256,512]{1,0:T(8,128)} %param.6) | copy-start | bytes 1572868
  21.0 12.7 %collective-permute-start = (f32[256,512]{1,0:T(8,128)S(1)}, f32[256,512]{1,0:T(8,128)S(1)}, u32[]{:S(2)}, u32[]{:S(2)}) collective-permute-start(f32[256,512]{1,0:T(8,128)S(1)} %get-tuple-element.40), channel_id=1, source_target_pairs={{0,2},{2,4},{4,6},{6,8},{8,10},{10,12},{12,14},{14,16},{16,18},{18... | collective-permute-start | bytes 1572872 | tf_op jit(solution)/shard_map/ppermute | solution.py:30
  22.7 11.2 %copy-start.23 = (f32[2,256,512]{2,1,0:T(8,128)S(1)}, f32[2,256,512]{2,1,0:T(8,128)}, u32[]{:S(2)}) copy-start(f32[2,256,512]{2,1,0:T(8,128)} %param.4) | copy-start | bytes 3145732
  22.7 11.2 %copy-start.27 = (f32[2,256,512]{2,1,0:T(8,128)S(1)}, f32[2,256,512]{2,1,0:T(8,128)}, u32[]{:S(2)}) copy-start(f32[2,256,512]{2,1,0:T(8,128)} %param.5) | copy-start | bytes 3145732
  37.0 57.7 %all-to-all-start = ((f32[2,256,512]{2,0,1:T(2,128)}), f32[2,256,512]{2,0,1:T(2,128)S(1)}, u32[]{:S(2)}, u32[]{:S(2)}) async-start(f32[2,256,512]{2,0,1:T(2,128)} %copy.58), calls=%async_computation | async-start | bytes 2097152 | tf_op jit(solution)/shard_map/all_to_all | solution.py:133
  95.8 15.4 %all-to-all-start.2 = ((f32[2,256,512]{2,1,0:T(8,128)}), f32[2,256,512]{2,1,0:T(8,128)S(1)}, u32[]{:S(2)}, u32[]{:S(2)}) async-start(f32[2,256,512]{2,1,0:T(8,128)} %broadcast_in_dim.5), calls=%async_computation.2 | async-start | bytes 2097152 | tf_op jit(solution)/shard_map/all_to_all | solution.py:62
  111.2 8.6 %copy-start.25 = (f32[2,256,512]{2,1,0:T(8,128)}, f32[2,256,512]{2,1,0:T(8,128)S(1)}, u32[]{:S(2)}) copy-start(f32[2,256,512]{2,1,0:T(8,128)S(1)} %all-to-all-done.2) | copy-start | bytes 3145732
  111.2 107.0 %all-to-all-start.1 = ((f32[32,2,1,16,512]{4,3,1,2,0:T(8,128)}), f32[32,2,1,16,512]{4,3,1,2,0:T(8,128)S(1)}, u32[]{:S(2)}, u32[]{:S(2)}) async-start(f32[32,2,1,16,512]{4,3,1,2,0:T(8,128)} %bitcast.19), calls=%async_computation.1 | async-start | bytes 4194304 | tf_op jit(solution)/shard_map/all_to_all | solution.py:55
  218.6 1.3 copy-start.22
  218.6 2.0 copy-start.1
  218.6 2.3 copy-start.6
  218.6 2.6 copy-start.11
  218.6 2.9 copy-start.16
  232.7 1.3 copy-start.21
  232.7 2.0 copy-start.2
  232.8 2.3 copy-start.7
  232.8 2.6 copy-start.12
  232.8 2.9 copy-start.17
  243.1 1.4 copy-start
  243.1 2.0 copy-start.3
  243.1 2.3 copy-start.8
  243.1 2.6 copy-start.13
  243.1 2.9 copy-start.18
  254.1 1.2 copy-start.4
  254.1 1.5 copy-start.9
  254.1 1.8 copy-start.14
  254.1 2.1 copy-start.19
  264.3 1.2 copy-start.5
  264.3 1.5 copy-start.10
  264.3 1.8 copy-start.15
  264.4 2.1 copy-start.20
  275.6 105.3 %all-to-all-start.3 = ((f32[32,2,1,1,16,512]{5,4,1,3,2,0:T(8,128)}), f32[32,2,1,1,16,512]{5,4,1,3,2,0:T(8,128)S(1)}, u32[]{:S(2)}, u32[]{:S(2)}) async-start(f32[32,2,1,1,16,512]{5,4,1,3,2,0:T(8,128)} %bitcast.114), calls=%async_computation.3 | async-start | bytes 4194304 | tf_op jit(solution)/shard_map/all_to_all | solution.py:55
  384.7 5.8 %copy-start.29 = (u32[128]{0:T(128)S(1)}, u32[128]{0:T(128)}, u32[]{:S(2)}) copy-start(u32[128]{0:T(128)} %constant.150) | copy-start | bytes 1540
  386.3 48.8 %copy-start.24 = (f32[2,256,512]{2,1,0:T(8,128)S(1)}, f32[2,256,512]{2,1,0:T(8,128)}, u32[]{:S(2)}) copy-start(f32[2,256,512]{2,1,0:T(8,128)} %param.4) | copy-start | bytes 3145732
  386.3 48.7 %all-to-all-start.4 = ((f32[32,16,512]{2,1,0:T(8,128)}), f32[32,16,512]{2,1,0:T(8,128)S(1)}, u32[]{:S(2)}, u32[]{:S(2)}) async-start(f32[32,16,512]{2,1,0:T(8,128)} %bitcast.76), calls=%async_computation.4 | async-start | bytes 2097152 | tf_op jit(solution)/shard_map/all_to_all | solution.py:198
where the time goes:
time: 442 us; the launch traced here: 436 us
  waiting for transfers between devices  286 us (65%)
  starting transfers between devices  58.2 us (13%)
  other arithmetic  47 us (11%)
  local copies, waits for them, and re-layouts  26.6 us (6%)
  between operations  8.78 us (2%)
  matrix products  5.51 us (1%)
    all_to_all x2, waiting for transfers between devices, exchange_both(): tiles = lax.all_to_all(tiles, axis, split_axis=0, concat_axis=0, tiled=True)  192 us
    all_to_all x1, waiting for transfers between devices, shards(): lax.all_to_all(scaled, 'tm', split_axis=1, concat_axis=0, tiled=True)  45.3 us
    all_to_all x1, waiting for transfers between devices, shards(): lax.all_to_all(correction, 'tm', split_axis=0, concat_axis=1, tiled=True)  38.6 us
    reduce_sum x6, other arithmetic, freq_norm(): return jnp.sum(values * values, axis=(0, 2, 3))  22.1 us
    unnamed x66, local copies, waits for them, and re-layouts  15.3 us
    ppermute x2, starting transfers between devices, extended(): lax.ppermute(lax.slice_in_dim(block, 0, width, axis=dim), axis, backward)  14.9 us
    all_to_all x2, starting transfers between devices, exchange_both(): tiles = lax.all_to_all(tiles, axis, split_axis=0, concat_axis=0, tiled=True)  13.6 us
    all_to_all x1, starting transfers between devices, shards(): lax.all_to_all(scaled, 'tm', split_axis=1, concat_axis=0, tiled=True)  12.4 us
  transfers between devices with their start and end apart: 10, of which 5 were waited for; matrix products, arithmetic and copies ran while one was open for 4% of the time, Pallas kernels for 0%

commit v1 on v0

v1 whole, which is shorter than its diff:
```python
import functools

import jax
import jax.numpy as jnp
import numpy as np
from jax import lax
from jax.experimental import pallas as pl
from jax.experimental.pallas import tpu as pltpu
from jax.sharding import PartitionSpec as P

circulant_alpha = 0.05
time_step = 0.5
rms_eps = 1e-06
MESH = pl.DeviceIdType.MESH


def rfft_list(x):
    n = len(x)
    if n == 1:
        return [(x[0], None)]
    even, odd = rfft_list(x[0::2]), rfft_list(x[1::2])
    half = n // 2
    out = [None] * (half + 1)
    out[0] = (even[0][0] + odd[0][0], None)
    out[half] = (even[0][0] - odd[0][0], None)
    for k in range(1, half // 2 + 1):
        if 2 * k == half:
            out[k] = (even[k][0], -odd[k][0])
            continue
        angle = 2.0 * np.pi * k / n
        cos, sin = float(np.cos(angle)), float(np.sin(angle))
        o_re, o_im = odd[k]
        if 8 * k == n:
            t_re, t_im = (o_re + o_im) * cos, (o_im - o_re) * cos
        else:
            t_re, t_im = o_re * cos + o_im * sin, o_im * cos - o_re * sin
        e_re, e_im = even[k]
        out[k] = (e_re + t_re, e_im + t_im)
        out[half - k] = (e_re - t_re, t_im - e_im)
    return out


def irfft_list(freq):
    half = len(freq) - 1
    n = 2 * half
    if n == 2:
        return [freq[0][0] + freq[1][0], freq[0][0] - freq[1][0]]
    even, odd = [None] * (half // 2 + 1), [None] * (half // 2 + 1)
    even[0] = (freq[0][0] + freq[half][0], None)
    odd[0] = (freq[0][0] - freq[half][0], None)
    for k in range(1, half // 2 + 1):
        if 2 * k == half:
            even[k] = (freq[k][0] + freq[k][0], None)
            odd[k] = (-(freq[k][1] + freq[k][1]), None)
            continue
        angle = 2.0 * np.pi * k / n
        cos, sin = float(np.cos(angle)), float(np.sin(angle))
        a_re, a_im = freq[k]
        b_re, b_im = freq[half - k]
        even[k] = (a_re + b_re, a_im - b_im)
        d_re, d_im = a_re - b_re, a_im + b_im
        if 8 * k == n:
            odd[k] = ((d_re - d_im) * cos, (d_re + d_im) * cos)
        else:
            odd[k] = (d_re * cos - d_im * sin, d_im * cos + d_re * sin)
    even_out, odd_out = irfft_list(even), irfft_list(odd)
    out = [None] * n
    out[0::2], out[1::2] = even_out, odd_out
    return out


def two_sum(a, b):
    s = a + b
    v = s - a
    return s, (a - (s - v)) + (b - v)


def quick_sum(a, b):
    s = a + b
    return s, b - (s - a)


def split(a):
    t = 4097.0 * a
    hi = t - (t - a)
    return hi, a - hi


def two_prod(a, b):
    p = a * b
    ah, al = split(a)
    bh, bl = split(b)
    return p, ((ah * bh - p) + ah * bl + al * bh) + al * bl


def pair_add(x, y):
    s, e = two_sum(x[0], y[0])
    return quick_sum(s, e + (x[1] + y[1]))


def pair_neg(x):
    return (-x[0], -x[1])


def pair_mul(x, y):
    p, e = two_prod(x[0], y[0])
    return quick_sum(p, e + (x[0] * y[1] + x[1] * y[0]))


def pair_div(x, y):
    q = x[0] / y[0]
    rest = pair_add(x, pair_neg(pair_mul((q, jnp.zeros_like(q)), y)))
    return quick_sum(q, rest[0] / y[0])


def krylov_weights(mu):
    one = (jnp.ones_like(mu[0][0]), jnp.zeros_like(mu[0][0]))
    zero = jnp.zeros_like(mu[0][0])
    inv0 = pair_div(one, mu[0])
    t1 = pair_div(mu[0], mu[1])
    t2 = pair_mul(t1, t1)
    t3 = pair_mul(t2, t1)
    t4 = pair_mul(t2, t2)
    t5 = pair_mul(t4, t1)
    m2, m3, m4, m5 = (
        pair_mul(pair_mul(mu[k], inv0), t) for k, t in ((2, t2), (3, t3), (4, t4), (5, t5))
    )
    tiny = 2.0**-32
    gain0 = pair_add(m2, pair_neg(one))
    den1 = pair_add(m3, pair_neg(pair_mul(m2, m2)))
    ok1 = (gain0[0] > tiny) & (den1[0] > tiny * m3[0])

    def kept(ok, x, other):
        return (jnp.where(ok, x[0], other), jnp.where(ok, x[1], 0.0))

    rate1 = kept(ok1, pair_div(kept(ok1, gain0, 0.0), kept(ok1, den1, 1.0)), 0.0)
    mid = pair_add(one, pair_mul(rate1, m2))
    inner = pair_add(pair_add(m2, pair_neg(pair_mul(mid, m3))), pair_mul(rate1, m4))
    size = m2[0] + mid[0] * m3[0] + rate1[0] * m4[0]
    ok2 = ok1 & (inner[0] > tiny * size)
    gamma2 = pair_mul(rate1, kept(ok2, inner, 0.0))
    gain1 = pair_div(gamma2, kept(ok1, gain0, 1.0))
    base = pair_add(one, pair_mul(gain1, m2))
    slope = pair_add(mid, gain1)
    inner2 = pair_add(
        pair_add(pair_mul(base, m3), pair_neg(pair_mul(slope, m4))), pair_mul(rate1, m5)
    )
    size2 = base[0] * m3[0] + slope[0] * m4[0] + rate1[0] * m5[0]
    ok3 = ok2 & (inner2[0] > tiny * size2)
    ratio = kept(ok2, inner, 0.0)
    rate2 = pair_div(ratio, kept(ok3, inner2, 1.0))
    rate2 = jnp.where(ok3, rate2[0], zero)
    w0 = mid[0] + rate2 * base[0]
    w1 = -(rate1[0] + rate2 * slope[0])
    w2 = rate2 * rate1[0]
    return w0 * t1[0], w1 * t2[0], w2 * t3[0]


def kernel(
    count,
    cells,
    it_hbm,
    fo_hbm,
    init_hbm,
    di_hbm,
    tab,
    out_ref,
    rms_ref,
    u_ext,
    force,
    before,
    d_ext,
    res,
    by_cell,
    spec,
    v0_ref,
    v1_ref,
    v2_ref,
    corr,
    back,
    weights,
    mom,
    coef,
    ar_send,
    ar_all,
    sq_send,
    sq_recv,
    load_sem,
    prev_sem,
    rim_send,
    rim_recv,
    a_send,
    a_recv,
    h_send,
    h_recv,
    m_send,
    m_recv,
    b_send,
    b_recv,
):
    t = lax.axis_index("tm")
    c = lax.axis_index("rows")
    me = c * count + t
    total = 2 * count
    length = 2 * count
    pairs = length // 2
    rows = force.shape[1]
    cols = force.shape[2]
    slab = rows // count
    tiles = cols // 128

    def pos(i):
        return {"tm": lax.rem(i, count), "rows": i // count}

    barrier = pltpu.get_barrier_semaphore()

    def greet(k, carry):
        pl.semaphore_signal(
            barrier, inc=1, device_id=pos(lax.rem(me + k, total)), device_id_type=MESH
        )
        return carry

    lax.fori_loop(1, total, greet, 0)

    loads = [
        pltpu.make_async_copy(di_hbm, d_ext.at[pl.ds(16, rows)], load_sem.at[0]),
        pltpu.make_async_copy(it_hbm, u_ext.at[:, pl.ds(8, rows)], load_sem.at[1]),
        pltpu.make_async_copy(fo_hbm, force, load_sem.at[2]),
    ]
    for load in loads:
        load.start()
    u_ext[:, pl.ds(pl.multiple_of(c * (rows + 8), 8), 8), :] = jnp.zeros((2, 8, cols), jnp.float32)
    pl.semaphore_wait(barrier, total - 1)

    partner = {"rows": 1 - c}
    rims = [
        pltpu.make_async_remote_copy(
            src_ref=di_hbm.at[pl.ds(pl.multiple_of((1 - c) * (rows - 16), 8), 16)],
            dst_ref=d_ext.at[pl.ds(pl.multiple_of(c * (rows + 16), 8), 16)],
            send_sem=rim_send.at[0],
            recv_sem=rim_recv.at[0],
            device_id=partner,
            device_id_type=MESH,
        ),
        pltpu.make_async_remote_copy(
            src_ref=it_hbm.at[:, pl.ds(pl.multiple_of((1 - c) * (rows - 8), 8), 8)],
            dst_ref=u_ext.at[:, pl.ds(pl.multiple_of(c * (rows + 8), 8), 8)],
            send_sem=rim_send.at[1],
            recv_sem=rim_recv.at[1],
            device_id=partner,
            device_id_type=MESH,
        ),
    ]
    for rim in rims:
        rim.start()

    onward = pltpu.make_async_remote_copy(
        src_ref=it_hbm.at[1],
        dst_ref=before,
        send_sem=prev_sem.at[0],
        recv_sem=prev_sem.at[1],
        device_id={"tm": lax.rem(t + 1, count)},
        device_id_type=MESH,
    )
    first = pltpu.make_async_copy(init_hbm, before, prev_sem.at[2])

    @pl.when(t < count - 1)
    def _():
        onward.start()

    @pl.when(t == 0)
    def _():
        first.start()

    for load in loads:
        load.wait()
    edge = jnp.where(c == 0, d_ext[16:24, :][:1], d_ext[rows + 8 : rows + 16, :][7:8])
    d_ext[pl.ds(pl.multiple_of(c * (rows + 16), 8), 16), :] = jnp.broadcast_to(edge, (16, cols))
    for rim in rims:
        rim.wait_recv()

    def lane_of(shape):
        return lax.broadcasted_iota(jnp.int32, shape, 1)

    def residual(step, dest):
        start = pl.multiple_of(dest * slab, slab)
        tall = slab + 16
        u = u_ext[step, pl.ds(start, tall), :]
        d = d_ext[pl.ds(pl.multiple_of(start + 8, 8), tall), :]
        lane = lane_of((slab, cols))
        mid = slice(8, slab + 8)
        uc, dc = u[mid], d[mid]
        u_n, u_s = pltpu.roll(u, 1, 0)[mid], pltpu.roll(u, tall - 1, 0)[mid]
        d_n, d_s = pltpu.roll(d, 1, 0)[mid], pltpu.roll(d, tall - 1, 0)[mid]
        u_w = jnp.where(lane == 0, 0.0, pltpu.roll(uc, 1, 1))
        u_e = jnp.where(lane == cols - 1, 0.0, pltpu.roll(uc, cols - 1, 1))
        d_w = jnp.where(lane == 0, dc, pltpu.roll(dc, 1, 1))
        d_e = jnp.where(lane == cols - 1, dc, pltpu.roll(dc, cols - 1, 1))
        spread = (
            (dc + d_n) * (uc - u_n)
            + (dc + d_s) * (uc - u_s)
            + (dc + d_w) * (uc - u_w)
            + (dc + d_e) * (uc - u_e)
        )
        if step == 0:
            prev = before[pl.ds(start, slab), :]
        else:
            prev = u_ext[step - 1, pl.ds(pl.multiple_of(start + 8, 8), slab), :]
        value = time_step * force[step, pl.ds(start, slab), :] + prev - uc
        return value - (0.5 * time_step) * spread

    def squares(value):
        sq = value * value
        folded = sq[0:8]
        for i in range(1, slab // 8):
            folded = folded + sq[8 * i : 8 * i + 8]
        total_sq = folded[:, 0:128]
        for i in range(1, tiles):
            total_sq = total_sq + folded[:, 128 * i : 128 * i + 128]
        return total_sq

    def peer(k):
        far = count // 2 - (k + 1) // 2
        return lax.rem(t + jnp.where(lax.rem(k, 2) == 1, far, count - far), count)

    def forward(step, k):
        dest = peer(k)
        block = pl.ds(pl.multiple_of(dest * slab, slab), slab)
        return pltpu.make_async_remote_copy(
            src_ref=res.at[step, block],
            dst_ref=by_cell.at[2 * t + step],
            send_sem=a_send.at[step, k],
            recv_sem=a_recv.at[step, t],
            device_id={"tm": dest},
            device_id_type=MESH,
        )

    for step in (1, 0):
        if step == 0:

            @pl.when(t > 0)
            def _():
                onward.wait_recv()

            @pl.when(t == 0)
            def _():
                first.wait()

        growth = tab[2 * t + step]

        def send_one(k, acc):
            dest = peer(k)
            value = residual(step, dest)
            res[step, pl.ds(pl.multiple_of(dest * slab, slab), slab), :] = value * growth
            forward(step, k).start()
            return acc + squares(value)

        acc = lax.fori_loop(0, count - 1, send_one, jnp.zeros((8, 128), jnp.float32))
        value = residual(step, t)
        by_cell[2 * t + step] = value * growth
        sq_send[step] = acc + squares(value)

    sq_copy = pltpu.make_async_remote_copy(
        src_ref=sq_send,
        dst_ref=sq_recv,
        send_sem=rim_send.at[2],
        recv_sem=rim_recv.at[2],
        device_id=partner,
        device_id_type=MESH,
    )
    sq_copy.start()

    d = d_ext[pl.ds(pl.multiple_of(t * slab, slab), slab + 32), :]
    tall = slab + 16
    mid = slice(8, slab + 24)
    dc = d[mid]
    lane = lane_of((tall, cols))
    quarter = 0.5 * time_step
    w_n = quarter * (dc + pltpu.roll(d, 1, 0)[mid])
    w_s = quarter * (dc + pltpu.roll(d, slab + 31, 0)[mid])
    w_w = quarter * (dc + jnp.where(lane == 0, dc, pltpu.roll(dc, 1, 1)))
    w_e = quarter * (dc + jnp.where(lane == cols - 1, dc, pltpu.roll(dc, cols - 1, 1)))
    weights[0] = w_n + w_s + w_w + w_e
    weights[1] = w_n
    weights[2] = w_s
    weights[3] = jnp.where(lane == 0, 0.0, w_w)
    weights[4] = jnp.where(lane == cols - 1, 0.0, w_e)

    def arrived(k, carry):
        source = peer(k)
        for step in (0, 1):
            pltpu.make_async_remote_copy(
                src_ref=res.at[step, pl.ds(0, slab)],
                dst_ref=by_cell.at[2 * source + step],
                send_sem=a_send.at[step, k],
                recv_sem=a_recv.at[step, source],
                device_id={"tm": source},
                device_id_type=MESH,
            ).wait_recv()
        return carry

    lax.fori_loop(0, count - 1, arrived, 0)

    row_tiles = slab // 8

    def transform(p, carry):
        r = pl.multiple_of((p // tiles) * 8, 8)
        q = pl.multiple_of(lax.rem(p, tiles) * 128, 128)
        x = [by_cell[n, pl.ds(r, 8), pl.ds(q, 128)] for n in range(length)]
        f = rfft_list(x)
        here = (pl.ds(pl.multiple_of(r + 8, 8), 8), pl.ds(q, 128))
        spec[(0,) + here] = f[0][0]
        spec[(1,) + here] = f[pairs][0]
        for j in range(1, pairs):
            spec[(2 * j,) + here] = f[j][0]
            spec[(2 * j + 1,) + here] = f[j][1]
        return carry

    lax.fori_loop(0, row_tiles * tiles, transform, 0)

    north, south = pos(lax.rem(me + total - 1, total)), pos(lax.rem(me + 1, total))

    def halo(side, q):
        fields = pl.ds(2 * q, 2)
        if side == 0:
            src, dst, target = slab, 0, south
        else:
            src, dst, target = 8, slab + 8, north
        return pltpu.make_async_remote_copy(
            src_ref=spec.at[fields, pl.ds(src, 8)],
            dst_ref=spec.at[fields, pl.ds(dst, 8)],
            send_sem=h_send.at[side, q],
            recv_sem=h_recv.at[side, q],
            device_id=target,
            device_id_type=MESH,
        )

    def send_halo(q, carry):
        halo(0, q).start()
        halo(1, q).start()
        return carry

    lax.fori_loop(0, pairs, send_halo, 0)

    top = jnp.where(me == 0, 0.0, 1.0)
    bottom = jnp.where(me == total - 1, 0.0, 1.0)
    n_tr = row_tiles + 2
    sub = lax.broadcasted_iota(jnp.int32, (8, cols), 0)

    def spread_of(v, wanted):
        down = [pltpu.roll(x, 1, 0) for x in v]
        up = [pltpu.roll(x, 7, 0) for x in v]
        out = {}
        for i in wanted:
            v_n = jnp.where(sub == 0, down[max(i - 1, 0)], down[i])
            v_s = jnp.where(sub == 7, up[min(i + 1, n_tr - 1)], up[i])
            here = slice(8 * i, 8 * i + 8)
            out[i] = (
                weights[0, here, :] * v[i]
                - weights[1, here, :] * v_n
                - weights[2, here, :] * v_s
                - weights[3, here, :] * pltpu.roll(v[i], 1, 1)
                - weights[4, here, :] * pltpu.roll(v[i], cols - 1, 1)
            )
        return out

    def clip(i, x):
        if i == 0:
            return x * top
        if i == n_tr - 1:
            return x * bottom
        return x

    inner = range(1, n_tr - 1)

    def folded(v):
        acc = None
        for i in inner:
            sq = v[i] * v[i]
            for k in range(tiles):
                part = sq[:, 128 * k : 128 * k + 128]
                acc = part if acc is None else acc + part
        return jnp.sum(acc, axis=0, keepdims=True)

    def solve(q, carry):
        halo(0, q).wait_recv()
        halo(1, q).wait_recv()
        a_re, a_im, b = tab[2 * length + q], tab[2 * length + pairs + q], tab[2 * length + 2 * pairs + q]
        v = [
            [clip(i, spec[2 * q + part, 8 * i : 8 * i + 8, :]) for i in range(n_tr)]
            for part in (0, 1)
        ]
        for order in range(6):
            wanted = inner if order == 5 else range(n_tr)
            sign = b if order % 2 == 0 else -b
            k_re, k_im = spread_of(v[0], wanted), spread_of(v[1], wanted)
            new_re, new_im = [None] * n_tr, [None] * n_tr
            for i in wanted:
                new_re[i] = clip(i, a_re * v[0][i] + sign * v[1][i] + k_re[i])
                new_im[i] = clip(i, a_im * v[1][i] - sign * v[0][i] + k_im[i])
            v = [new_re, new_im]
            mom[2 * order, pl.ds(q, 1), :] = folded(v[0])
            mom[2 * order + 1, pl.ds(q, 1), :] = folded(v[1])
            if order % 2 == 0:
                keep = (v0_ref, v1_ref, v2_ref)[order // 2]
                for part in (0, 1):
                    for i in inner:
                        keep[2 * q + part, 8 * i - 8 : 8 * i, :] = v[part][i]
        return carry

    lax.fori_loop(0, pairs, solve, 0)

    row = lax.broadcasted_iota(jnp.int32, (pairs, 128), 0)
    lane8 = lax.broadcasted_iota(jnp.int32, (8, 128), 1)
    row8 = lax.broadcasted_iota(jnp.int32, (8, 128), 0)
    packed = [jnp.zeros((8, 128), jnp.float32), jnp.zeros((8, 128), jnp.float32)]

    def slot(k, g):
        return lane8 == (16 * row8 + 2 * k + g if g < 2 else 16 * k + 12)

    for k in range(6):
        re, im = mom[2 * k], mom[2 * k + 1]
        both = jnp.where(row == 0, re, re + im)
        for g in range(3):
            x = both[8 * g : 8 * g + 8] if g < 2 else im[0:8]
            big = 256.0 * jnp.max(x, axis=1, keepdims=True)
            hi = (x + big) - big
            lo = x - hi
            where = slot(k, g) if g < 2 else slot(k, g) & (row8 == 0)
            packed[0] = jnp.where(where, jnp.sum(hi, axis=1, keepdims=True), packed[0])
            packed[1] = jnp.where(where, jnp.sum(lo, axis=1, keepdims=True), packed[1])
    mine = jnp.concatenate([jnp.sum(x, axis=0, keepdims=True) for x in packed], axis=1)
    ar_send[...] = mine
    ar_all[me] = mine

    def share(k):
        return pltpu.make_async_remote_copy(
            src_ref=ar_send,
            dst_ref=ar_all.at[me],
            send_sem=m_send.at[k],
            recv_sem=m_recv.at[me],
            device_id=pos(lax.rem(me + k, total)),
            device_id_type=MESH,
        )

    def share_one(k, carry):
        share(k).start()
        return carry

    lax.fori_loop(1, total, share_one, 0)

    def shared(k, carry):
        source = lax.rem(me + k, total)
        pltpu.make_async_remote_copy(
            src_ref=ar_send,
            dst_ref=ar_all.at[source],
            send_sem=m_send.at[k],
            recv_sem=m_recv.at[source],
            device_id=pos(source),
            device_id_type=MESH,
        ).wait_recv()
        return carry

    lax.fori_loop(1, total, shared, 0)
    sums = [(ar_all[i][:, 0:128], ar_all[i][:, 128:256]) for i in range(total)]
    while len(sums) > 1:
        sums = [pair_add(sums[2 * i], sums[2 * i + 1]) for i in range(len(sums) // 2)]
    whole = [jnp.broadcast_to(x, (8, 128)) for x in sums[0]]
    mu = []
    for k in range(6):
        sides = []
        for x in whole:
            groups = [
                jnp.broadcast_to(
                    jnp.sum(jnp.where(slot(k, g), x, 0.0), axis=1, keepdims=True), (8, 128)
                )
                for g in range(3)
            ]
            sides.append(jnp.concatenate(groups, axis=0))
        mu.append(tuple(sides))
    for k, w in enumerate(krylov_weights(mu)):
        coef[k, 0] = w[0:pairs]
        coef[k, 1] = jnp.where(row == 0, w[pairs : pairs + 1], w[0:pairs])

    def restore(p, carry):
        r = pl.multiple_of((p // tiles) * 8, 8)
        q = pl.multiple_of(lax.rem(p, tiles) * 128, 128)
        here = (pl.ds(r, 8), pl.ds(q, 128))

        def field(f):
            j, part = f // 2, f % 2
            out = coef[0, part, j : j + 1, :] * v0_ref[(f,) + here]
            out = out + coef[1, part, j : j + 1, :] * v1_ref[(f,) + here]
            return out + coef[2, part, j : j + 1, :] * v2_ref[(f,) + here]

        freq = [(field(0), None)]
        freq += [(field(2 * j), field(2 * j + 1)) for j in range(1, pairs)]
        freq += [(field(1), None)]
        for n, x in enumerate(irfft_list(freq)):
            corr[(n,) + here] = x * tab[length + n]
        return carry

    lax.fori_loop(0, row_tiles * tiles, restore, 0)

    own = pl.ds(pl.multiple_of(t * slab, slab), slab)

    def send_back(k, carry):
        dest = peer(k)
        pltpu.make_async_remote_copy(
            src_ref=corr.at[pl.ds(2 * dest, 2)],
            dst_ref=back.at[:, own],
            send_sem=b_send.at[k],
            recv_sem=b_recv.at[t],
            device_id={"tm": dest},
            device_id_type=MESH,
        ).start()
        return carry

    lax.fori_loop(0, count - 1, send_back, 0)

    sq_copy.wait()
    rms = jnp.sqrt(
        jnp.sum(jnp.sum(sq_send[...] + sq_recv[...], axis=2, keepdims=True), axis=1, keepdims=True) / cells
        + rms_eps
    )
    rms_ref[...] = jnp.broadcast_to(rms[:, 0], (2, 128))

    def final(source, piece):
        block = pl.ds(pl.multiple_of(source * slab, slab), slab)
        ahead = pl.ds(pl.multiple_of(source * slab + 8, 8), slab)
        out_ref[:, block, :] = u_ext[:, ahead, :] + piece

    final(t, corr[pl.ds(2 * t, 2)])

    def returned(k, carry):
        source = peer(k)
        block = pl.ds(pl.multiple_of(source * slab, slab), slab)
        pltpu.make_async_remote_copy(
            src_ref=corr.at[pl.ds(0, 2)],
            dst_ref=back.at[:, block],
            send_sem=b_send.at[k],
            recv_sem=b_recv.at[source],
            device_id={"tm": source},
            device_id_type=MESH,
        ).wait_recv()
        final(source, back[:, block, :])
        return carry

    lax.fori_loop(0, count - 1, returned, 0)

    for rim in rims:
        rim.wait_send()

    @pl.when(t < count - 1)
    def _():
        onward.wait_send()

    def drain_peers(k, carry):
        forward(0, k).wait_send()
        forward(1, k).wait_send()
        pltpu.make_async_remote_copy(
            src_ref=corr.at[pl.ds(0, 2)],
            dst_ref=back.at[:, own],
            send_sem=b_send.at[k],
            recv_sem=b_recv.at[t],
            device_id={"tm": peer(k)},
            device_id_type=MESH,
        ).wait_send()
        return carry

    lax.fori_loop(0, count - 1, drain_peers, 0)

    def drain_halo(q, carry):
        halo(0, q).wait_send()
        halo(1, q).wait_send()
        return carry

    lax.fori_loop(0, pairs, drain_halo, 0)

    def drain_share(k, carry):
        share(k).wait_send()
        return carry

    lax.fori_loop(1, total, drain_share, 0)


def tables(length):
    pairs = length // 2
    n = np.arange(length)
    growth = np.exp(np.log(circulant_alpha) * n / length)
    root = np.exp(np.log(circulant_alpha) / length)
    j = np.arange(pairs)
    a_re = 1.0 - root * np.cos(2.0 * np.pi * j / length)
    a_im = a_re.copy()
    a_im[0] = 1.0 + root
    b = root * np.sin(2.0 * np.pi * j / length)
    return np.concatenate([growth, 1.0 / (length * growth), a_re, a_im, b]).astype(np.float32)


def shards(iterate, forcing, initial_state, diffusivity):
    steps, rows, cols = iterate.shape
    count = lax.axis_size("tm")
    halves = lax.axis_size("rows")
    length = steps * count
    assert steps == 2 and halves == 2
    slab = rows // count
    pairs = length // 2
    total = 2 * count
    cells = rows * halves * cols
    f32 = jnp.float32
    vmem = pltpu.VMEM
    dma = pltpu.SemaphoreType.DMA
    hbm = pl.BlockSpec(memory_space=pl.ANY)
    updated, rms = pl.pallas_call(
        functools.partial(kernel, count, cells),
        out_shape=(
            jax.ShapeDtypeStruct((steps, rows, cols), f32),
            jax.ShapeDtypeStruct((steps, 128), f32),
        ),
        in_specs=[hbm] * 4 + [pl.BlockSpec(memory_space=pltpu.SMEM)],
        out_specs=(pl.BlockSpec(memory_space=vmem), pl.BlockSpec(memory_space=vmem)),
        scratch_shapes=[
            vmem((steps, rows + 16, cols), f32),
            vmem((steps, rows, cols), f32),
            vmem((rows, cols), f32),
            vmem((rows + 32, cols), f32),
            vmem((steps, rows, cols), f32),
            vmem((length, slab, cols), f32),
            vmem((length, slab + 16, cols), f32),
            vmem((length, slab, cols), f32),
            vmem((length, slab, cols), f32),
            vmem((length, slab, cols), f32),
            vmem((length, slab, cols), f32),
            vmem((steps, rows, cols), f32),
            vmem((5, slab + 16, cols), f32),
            vmem((12, pairs, 128), f32),
            vmem((3, 2, pairs, 128), f32),
            vmem((1, 256), f32),
            vmem((total, 1, 256), f32),
            vmem((2, 8, 128), f32),
            vmem((2, 8, 128), f32),
            dma((3,)),
            dma((3,)),
            dma((3,)),
            dma((3,)),
            dma((2, count)),
            dma((2, count)),
            dma((2, pairs)),
            dma((2, pairs)),
            dma((total,)),
            dma((total,)),
            dma((count,)),
            dma((count,)),
        ],
        compiler_params=pltpu.CompilerParams(collective_id=0, has_side_effects=True),
        name="paradiag",
    )(iterate, forcing, initial_state, diffusivity, jnp.asarray(tables(length)))
    return updated, rms[:, 0]


def solution(mesh):
    placed = (
        P(("groups", "tm"), "rows", None),
        P(("groups", "tm"), "rows", None),
        P(("groups", "rows"), None),
        P(("groups", "rows"), None),
    )
    return jax.shard_map(
        shards,
        mesh=mesh,
        in_specs=placed,
        out_specs=(P(("groups", "tm"), "rows", None), P(("groups", "tm"))),
        check_vma=False,
    )
```

time: 442 us -> 157 us (0.36); the launches traced: 436 us -> 156 us
  waiting for transfers between devices: 286 us -> 0 us
  Pallas kernels: 0 us -> 152 us
  starting transfers between devices: 58.2 us -> 0 us
  other arithmetic: 47 us -> 0 us
  local copies, waits for them, and re-layouts: 26.6 us -> 3.55 us
  between operations: 8.78 us -> 0.65 us
  matrix products: 5.51 us -> 0 us
    all_to_all x5 -> x0, waiting for transfers between devices: 276 us -> none  [the longest x2 192 us: exchange_both(): tiles = lax.all_to_all(tiles, axis, split_axis=0, concat_axis=0, tiled=True)]
    pallas_call x0 -> x1, Pallas kernels: none -> 152 us  [shards(): pl.pallas_call(functools.partial(kernel, count, cells), out_shape=(jax.Sh...]
    all_to_all x5 -> x0, starting transfers between devices: 39.2 us -> none  [the longest x2 13.6 us: exchange_both(): tiles = lax.all_to_all(tiles, axis, split_axis=0, concat_axis=0, tiled=True)]
    reduce_sum x8 -> x0, other arithmetic: 23.3 us -> none  [the longest x6 22.1 us: freq_norm(): return jnp.sum(values * values, axis=(0, 2, 3))]
    ppermute x5 -> x0, starting transfers between devices: 19 us -> none  [the longest x2 14.9 us: extended(): lax.ppermute(lax.slice_in_dim(block, 0, width, axis=dim), axis, backward)]
    add x7 -> x0, other arithmetic: 15.8 us -> none  [the longest x2 6.7 us: apply_faces(): north_face + south_face + west_face + east_face]
    unnamed x66 -> x3, local copies, waits for them, and re-layouts: 15.3 us -> 2.93 us
    ppermute x5 -> x0, waiting for transfers between devices: 10.6 us -> none  [the longest x1 10.6 us: from_behind(): lax.ppermute(value, axis, [(source, source + steps) for source in range(i...]
  transfers between devices with their start and end apart: 10 -> 0, of which waited for: 5 -> 0; matrix products, arithmetic and copies ran while one was open for 4% -> 0% of each run, Pallas kernels for 0% -> 0%
where the time goes in v1:
time: 157 us; the launch traced here: 156 us
  Pallas kernels  152 us (97%)
  local copies, waits for them, and re-layouts  3.55 us (2%)
    pallas_call x1, Pallas kernels, shards(): pl.pallas_call(functools.partial(kernel, count, cells), out_shape=(jax.Sh...  152 us

profile of v1, /device:TPU:69, one launch (start us, length us, event | category | flops | bytes accessed | tf_op | source)
XLA Modules:
  0.0 156.4 jit_solution(10358775224925803619)
XLA Ops:
  0.6 152.2 %paradiag.1 = (f32[2,256,512]{2,1,0:T(8,128)}, f32[2,128]{1,0:T(2,128)}) custom-call(f32[2,256,512]{2,1,0:T(8,128)} %it_hbm.1, f32[2,256,512]{2,1,0:T(8,128)} %fo_hbm.1, f32[256,512]{1,0:T(8,128)} %init_hbm.1, f32[256,512]{1,0:T(8,128)} %di_hbm.1, f32[112]{0:T(128)} %constant.2.clone.tab), custom_call_target="tpu_custom_call" | custom-call | tf_op jit(solution)/shard_map/paradiag/pallas_call | solution.py:714
  152.9 0.0 copy-start
  152.9 0.7 copy-done
  153.6 0.6 slice_reduce_fusion
  154.2 2.3 %copy.8 = f32[2,256,512]{2,1,0:T(8,128)} copy(f32[2,256,512]{2,1,0:T(8,128)} %get-tuple-element.8) | data formatting | bytes 2097152
Async XLA Ops:
  152.9 0.7 copy-start

commit v2 on v1

--- a/solution.py
+++ b/solution.py
@@ -197,6 +197,8 @@
     m_recv,
     b_send,
     b_recv,
+    from_left,
+    from_right,
 ):
     t = lax.axis_index("tm")
     c = lax.axis_index("rows")
@@ -214,13 +216,10 @@
 
     barrier = pltpu.get_barrier_semaphore()
 
-    def greet(k, carry):
-        pl.semaphore_signal(
-            barrier, inc=1, device_id=pos(lax.rem(me + k, total)), device_id_type=MESH
-        )
-        return carry
-
-    lax.fori_loop(1, total, greet, 0)
+    right, left = {"tm": lax.rem(t + 1, count)}, {"tm": lax.rem(t + count - 1, count)}
+    partner = {"rows": 1 - c}
+    for neighbour in (left, right, partner):
+        pl.semaphore_signal(barrier, inc=1, device_id=neighbour, device_id_type=MESH)
 
     loads = [
         pltpu.make_async_copy(di_hbm, d_ext.at[pl.ds(16, rows)], load_sem.at[0]),
@@ -230,9 +229,26 @@
     for load in loads:
         load.start()
     u_ext[:, pl.ds(pl.multiple_of(c * (rows + 8), 8), 8), :] = jnp.zeros((2, 8, cols), jnp.float32)
-    pl.semaphore_wait(barrier, total - 1)
-
-    partner = {"rows": 1 - c}
+    pl.semaphore_wait(barrier, 3)
+
+    onward = pltpu.make_async_remote_copy(
+        src_ref=it_hbm.at[1],
+        dst_ref=before,
+        send_sem=prev_sem.at[0],
+        recv_sem=prev_sem.at[1],
+        device_id=right,
+        device_id_type=MESH,
+    )
+    first = pltpu.make_async_copy(init_hbm, before, prev_sem.at[2])
+
+    @pl.when(t < count - 1)
+    def _():
+        onward.start()
+
+    @pl.when(t == 0)
+    def _():
+        first.start()
+
     rims = [
         pltpu.make_async_remote_copy(
             src_ref=di_hbm.at[pl.ds(pl.multiple_of((1 - c) * (rows - 16), 8), 16)],
@@ -253,24 +269,6 @@
     ]
     for rim in rims:
         rim.start()
-
-    onward = pltpu.make_async_remote_copy(
-        src_ref=it_hbm.at[1],
-        dst_ref=before,
-        send_sem=prev_sem.at[0],
-        recv_sem=prev_sem.at[1],
-        device_id={"tm": lax.rem(t + 1, count)},
-        device_id_type=MESH,
-    )
-    first = pltpu.make_async_copy(init_hbm, before, prev_sem.at[2])
-
-    @pl.when(t < count - 1)
-    def _():
-        onward.start()
-
-    @pl.when(t == 0)
-    def _():
-        first.start()
 
     for load in loads:
         load.wait()
@@ -323,42 +321,59 @@
         far = count // 2 - (k + 1) // 2
         return lax.rem(t + jnp.where(lax.rem(k, 2) == 1, far, count - far), count)
 
-    def forward(step, k):
-        dest = peer(k)
+    def forward(step, dest):
         block = pl.ds(pl.multiple_of(dest * slab, slab), slab)
         return pltpu.make_async_remote_copy(
             src_ref=res.at[step, block],
             dst_ref=by_cell.at[2 * t + step],
-            send_sem=a_send.at[step, k],
+            send_sem=a_send.at[step, dest],
             recv_sem=a_recv.at[step, t],
             device_id={"tm": dest},
             device_id_type=MESH,
         )
 
-    for step in (1, 0):
-        if step == 0:
-
-            @pl.when(t > 0)
-            def _():
-                onward.wait_recv()
-
-            @pl.when(t == 0)
-            def _():
-                first.wait()
-
-        growth = tab[2 * t + step]
-
-        def send_one(k, acc):
-            dest = peer(k)
-            value = residual(step, dest)
-            res[step, pl.ds(pl.multiple_of(dest * slab, slab), slab), :] = value * growth
-            forward(step, k).start()
-            return acc + squares(value)
-
-        acc = lax.fori_loop(0, count - 1, send_one, jnp.zeros((8, 128), jnp.float32))
+    def send_one(step, dest, acc):
+        value = residual(step, dest)
+        res[step, pl.ds(pl.multiple_of(dest * slab, slab), slab), :] = value * tab[2 * t + step]
+        forward(step, dest).start()
+        return acc + squares(value)
+
+    def keep_own(step, acc):
         value = residual(step, t)
-        by_cell[2 * t + step] = value * growth
+        by_cell[2 * t + step] = value * tab[2 * t + step]
         sq_send[step] = acc + squares(value)
+
+    def pass_tokens():
+        pl.semaphore_signal(from_left, inc=1, device_id=right, device_id_type=MESH)
+        pl.semaphore_signal(from_right, inc=1, device_id=left, device_id_type=MESH)
+
+    def widen(k, acc):
+        pass_tokens()
+        acc = send_one(1, lax.rem(t + k, count), acc)
+        acc = send_one(1, lax.rem(t + count - k, count), acc)
+        pl.semaphore_wait(from_left, 1)
+        pl.semaphore_wait(from_right, 1)
+        return acc
+
+    acc = lax.fori_loop(1, count // 2, widen, jnp.zeros((8, 128), jnp.float32))
+    pass_tokens()
+    acc = send_one(1, lax.rem(t + count // 2, count), acc)
+    keep_own(1, acc)
+
+    @pl.when(t > 0)
+    def _():
+        onward.wait_recv()
+
+    @pl.when(t == 0)
+    def _():
+        first.wait()
+
+    acc = lax.fori_loop(
+        0, count - 1, lambda k, acc: send_one(0, peer(k), acc), jnp.zeros((8, 128), jnp.float32)
+    )
+    keep_own(0, acc)
+    pl.semaphore_wait(from_left, 1)
+    pl.semaphore_wait(from_right, 1)
 
     sq_copy = pltpu.make_async_remote_copy(
         src_ref=sq_send,
@@ -392,7 +407,7 @@
             pltpu.make_async_remote_copy(
                 src_ref=res.at[step, pl.ds(0, slab)],
                 dst_ref=by_cell.at[2 * source + step],
-                send_sem=a_send.at[step, k],
+                send_sem=a_send.at[step, source],
                 recv_sem=a_recv.at[step, source],
                 device_id={"tm": source},
                 device_id_type=MESH,
@@ -656,8 +671,8 @@
         onward.wait_send()
 
     def drain_peers(k, carry):
-        forward(0, k).wait_send()
-        forward(1, k).wait_send()
+        forward(0, peer(k)).wait_send()
+        forward(1, peer(k)).wait_send()
         pltpu.make_async_remote_copy(
             src_ref=corr.at[pl.ds(0, 2)],
             dst_ref=back.at[:, own],
@@ -714,8 +729,8 @@
     updated, rms = pl.pallas_call(
         functools.partial(kernel, count, cells),
         out_shape=(
-            jax.ShapeDtypeStruct((steps, rows, cols), f32),
-            jax.ShapeDtypeStruct((steps, 128), f32),
+            vmem((steps, rows, cols), f32),
+            vmem((steps, 128), f32),
         ),
         in_specs=[hbm] * 4 + [pl.BlockSpec(memory_space=pltpu.SMEM)],
         out_specs=(pl.BlockSpec(memory_space=vmem), pl.BlockSpec(memory_space=vmem)),
@@ -751,6 +766,8 @@
             dma((total,)),
             dma((count,)),
             dma((count,)),
+            pltpu.SemaphoreType.REGULAR,
+            pltpu.SemaphoreType.REGULAR,
         ],
         compiler_params=pltpu.CompilerParams(collective_id=0, has_side_effects=True),
         name="paradiag",

time: 157 us -> 149 us (0.949)
  Pallas kernels: 152 us -> 147 us
  local copies, waits for them, and re-layouts: 3.55 us -> 1.6 us
    pallas_call x1, Pallas kernels: 152 us -> 147 us  [shards(): pl.pallas_call(functools.partial(kernel, count, cells), out_shape=(vmem((...]
    unnamed x3 -> x1, local copies, waits for them, and re-layouts: 2.93 us -> 0.97 us
where the time goes in v2:
time: 149 us
  Pallas kernels  147 us (99%)
  local copies, waits for them, and re-layouts  1.6 us (1%)
    pallas_call x1, Pallas kernels, shards(): pl.pallas_call(functools.partial(kernel, count, cells), out_shape=(vmem((...  147 us

profile of v2, /device:TPU:69, one launch (start us, length us, event | category | flops | bytes accessed | tf_op | source)
XLA Modules:
  0.0 149.4 jit_solution(9035171919929829112)
XLA Ops:
  0.6 147.1 %paradiag.1 = (f32[2,256,512]{2,1,0:T(8,128)S(1)}, f32[2,128]{1,0:T(2,128)S(1)}) custom-call(f32[2,256,512]{2,1,0:T(8,128)} %it_hbm.1, f32[2,256,512]{2,1,0:T(8,128)} %fo_hbm.1, f32[256,512]{1,0:T(8,128)} %init_hbm.1, f32[256,512]{1,0:T(8,128)} %di_hbm.1, f32[112]{0:T(128)} %constant.2.clone.tab), custom_call_target="tpu_custom_call" | custom-call | tf_op jit(solution)/shard_map/paradiag/pallas_call | solution.py:729
  147.8 1.0 copy.8
  148.7 0.6 slice_reduce_fusion

commit v3 on v2

--- a/solution.py
+++ b/solution.py
@@ -176,6 +176,7 @@
     v0_ref,
     v1_ref,
     v2_ref,
+    xs,
     corr,
     back,
     weights,
@@ -193,6 +194,10 @@
     a_recv,
     h_send,
     h_recv,
+    x_send,
+    x_recv,
+    y_send,
+    y_recv,
     m_send,
     m_recv,
     b_send,
@@ -202,17 +207,17 @@
 ):
     t = lax.axis_index("tm")
     c = lax.axis_index("rows")
-    me = c * count + t
-    total = 2 * count
     length = 2 * count
     pairs = length // 2
+    share = pairs // 2
     rows = force.shape[1]
     cols = force.shape[2]
-    slab = rows // count
+    half = count // 2
+    slab = rows // half
+    piece = slab // 2
     tiles = cols // 128
-
-    def pos(i):
-        return {"tm": lax.rem(i, count), "rows": i // count}
+    home = t // half
+    place = lax.rem(t, half)
 
     barrier = pltpu.get_barrier_semaphore()
 
@@ -222,7 +227,7 @@
         pl.semaphore_signal(barrier, inc=1, device_id=neighbour, device_id_type=MESH)
 
     loads = [
-        pltpu.make_async_copy(di_hbm, d_ext.at[pl.ds(16, rows)], load_sem.at[0]),
+        pltpu.make_async_copy(di_hbm, d_ext.at[pl.ds(pl.multiple_of(16 + rows * c, 8), rows)], load_sem.at[0]),
         pltpu.make_async_copy(it_hbm, u_ext.at[:, pl.ds(8, rows)], load_sem.at[1]),
         pltpu.make_async_copy(fo_hbm, force, load_sem.at[2]),
     ]
@@ -251,8 +256,8 @@
 
     rims = [
         pltpu.make_async_remote_copy(
-            src_ref=di_hbm.at[pl.ds(pl.multiple_of((1 - c) * (rows - 16), 8), 16)],
-            dst_ref=d_ext.at[pl.ds(pl.multiple_of(c * (rows + 16), 8), 16)],
+            src_ref=di_hbm,
+            dst_ref=d_ext.at[pl.ds(pl.multiple_of(16 + rows * c, 8), rows)],
             send_sem=rim_send.at[0],
             recv_sem=rim_recv.at[0],
             device_id=partner,
@@ -272,19 +277,19 @@
 
     for load in loads:
         load.wait()
-    edge = jnp.where(c == 0, d_ext[16:24, :][:1], d_ext[rows + 8 : rows + 16, :][7:8])
-    d_ext[pl.ds(pl.multiple_of(c * (rows + 16), 8), 16), :] = jnp.broadcast_to(edge, (16, cols))
     for rim in rims:
         rim.wait_recv()
+    d_ext[0:16, :] = jnp.broadcast_to(d_ext[16:24, :][:1], (16, cols))
+    last = 2 * rows + 16
+    d_ext[last : last + 16, :] = jnp.broadcast_to(d_ext[last - 8 : last, :][7:8], (16, cols))
 
     def lane_of(shape):
         return lax.broadcasted_iota(jnp.int32, shape, 1)
 
-    def residual(step, dest):
-        start = pl.multiple_of(dest * slab, slab)
+    def residual(step, start):
         tall = slab + 16
         u = u_ext[step, pl.ds(start, tall), :]
-        d = d_ext[pl.ds(pl.multiple_of(start + 8, 8), tall), :]
+        d = d_ext[pl.ds(pl.multiple_of(rows * c + start + 8, 8), tall), :]
         lane = lane_of((slab, cols))
         mid = slice(8, slab + 8)
         uc, dc = u[mid], d[mid]
@@ -317,48 +322,64 @@
             total_sq = total_sq + folded[:, 128 * i : 128 * i + 128]
         return total_sq
 
+    def forward(step, dest, core):
+        start = pl.multiple_of(lax.rem(dest, half) * slab + piece * core, 8)
+        return pltpu.make_async_remote_copy(
+            src_ref=res.at[step, pl.ds(start, piece)],
+            dst_ref=by_cell.at[2 * t + step],
+            send_sem=a_send.at[step, lax.rem(dest, half), core],
+            recv_sem=a_recv.at[step, t],
+            device_id={"tm": dest, "rows": core},
+            device_id_type=MESH,
+        )
+
+    def chip(j):
+        return half * c + lax.rem(t + half // 2 + j, half)
+
+    def elsewhere(dest, core):
+        return jnp.logical_or(dest != t, core != c)
+
     def peer(k):
         far = count // 2 - (k + 1) // 2
         return lax.rem(t + jnp.where(lax.rem(k, 2) == 1, far, count - far), count)
 
-    def forward(step, dest):
-        block = pl.ds(pl.multiple_of(dest * slab, slab), slab)
-        return pltpu.make_async_remote_copy(
-            src_ref=res.at[step, block],
-            dst_ref=by_cell.at[2 * t + step],
-            send_sem=a_send.at[step, dest],
-            recv_sem=a_recv.at[step, t],
-            device_id={"tm": dest},
-            device_id_type=MESH,
-        )
-
-    def send_one(step, dest, acc):
-        value = residual(step, dest)
-        res[step, pl.ds(pl.multiple_of(dest * slab, slab), slab), :] = value * tab[2 * t + step]
-        forward(step, dest).start()
-        return acc + squares(value)
-
-    def keep_own(step, acc):
-        value = residual(step, t)
-        by_cell[2 * t + step] = value * tab[2 * t + step]
-        sq_send[step] = acc + squares(value)
-
-    def pass_tokens():
+    def make(step, dest):
+        start = pl.multiple_of(lax.rem(dest, half) * slab, slab)
+        value = residual(step, start)
+        res[step, pl.ds(start, slab), :] = value * tab[2 * t + step]
+        sq_send[step] = sq_send[step] + squares(value)
+
+    def send_one(step, dest):
+        @pl.when(dest // half == c)
+        def _():
+            make(step, dest)
+            forward(step, dest, 0).start()
+            forward(step, dest, 1).start()
+
+    def send_home(step):
+        @pl.when(home == c)
+        def _():
+            make(step, t)
+            start = pl.multiple_of(place * slab + piece * c, 8)
+            by_cell[2 * t + step] = res[step, pl.ds(start, piece), :]
+            forward(step, t, 1 - c).start()
+
+    def widen(k, carry):
         pl.semaphore_signal(from_left, inc=1, device_id=right, device_id_type=MESH)
         pl.semaphore_signal(from_right, inc=1, device_id=left, device_id_type=MESH)
-
-    def widen(k, acc):
-        pass_tokens()
-        acc = send_one(1, lax.rem(t + k, count), acc)
-        acc = send_one(1, lax.rem(t + count - k, count), acc)
         pl.semaphore_wait(from_left, 1)
         pl.semaphore_wait(from_right, 1)
-        return acc
-
-    acc = lax.fori_loop(1, count // 2, widen, jnp.zeros((8, 128), jnp.float32))
-    pass_tokens()
-    acc = send_one(1, lax.rem(t + count // 2, count), acc)
-    keep_own(1, acc)
+        send_one(1, lax.rem(t + k, count))
+
+        @pl.when(k < half)
+        def _():
+            send_one(1, lax.rem(t + count - k, count))
+
+        return carry
+
+    sq_send[...] = jnp.zeros((2, 8, 128), jnp.float32)
+    lax.fori_loop(1, half + 1, widen, 0)
+    send_home(1)
 
     @pl.when(t > 0)
     def _():
@@ -368,12 +389,12 @@
     def _():
         first.wait()
 
-    acc = lax.fori_loop(
-        0, count - 1, lambda k, acc: send_one(0, peer(k), acc), jnp.zeros((8, 128), jnp.float32)
-    )
-    keep_own(0, acc)
-    pl.semaphore_wait(from_left, 1)
-    pl.semaphore_wait(from_right, 1)
+    def send_far(k, carry):
+        send_one(0, peer(k))
+        return carry
+
+    lax.fori_loop(0, count - 1, send_far, 0)
+    send_home(0)
 
     sq_copy = pltpu.make_async_remote_copy(
         src_ref=sq_send,
@@ -390,79 +411,100 @@
     mid = slice(8, slab + 24)
     dc = d[mid]
     lane = lane_of((tall, cols))
+    line = lax.broadcasted_iota(jnp.int32, (tall, cols), 0)
+    outside = ((t == 0) & (line < 8)) | ((t == count - 1) & (line >= slab + 8))
     quarter = 0.5 * time_step
     w_n = quarter * (dc + pltpu.roll(d, 1, 0)[mid])
     w_s = quarter * (dc + pltpu.roll(d, slab + 31, 0)[mid])
     w_w = quarter * (dc + jnp.where(lane == 0, dc, pltpu.roll(dc, 1, 1)))
     w_e = quarter * (dc + jnp.where(lane == cols - 1, dc, pltpu.roll(dc, cols - 1, 1)))
     weights[0] = w_n + w_s + w_w + w_e
-    weights[1] = w_n
-    weights[2] = w_s
+    weights[1] = jnp.where(outside, 0.0, w_n)
+    weights[2] = jnp.where(outside, 0.0, w_s)
     weights[3] = jnp.where(lane == 0, 0.0, w_w)
     weights[4] = jnp.where(lane == cols - 1, 0.0, w_e)
 
+    def arrival(step, source):
+        return pltpu.make_async_remote_copy(
+            src_ref=res.at[step, pl.ds(0, piece)],
+            dst_ref=by_cell.at[2 * source + step],
+            send_sem=a_send.at[step, 0, 0],
+            recv_sem=a_recv.at[step, source],
+            device_id={"tm": source},
+            device_id_type=MESH,
+        )
+
     def arrived(k, carry):
-        source = peer(k)
         for step in (0, 1):
-            pltpu.make_async_remote_copy(
-                src_ref=res.at[step, pl.ds(0, slab)],
-                dst_ref=by_cell.at[2 * source + step],
-                send_sem=a_send.at[step, source],
-                recv_sem=a_recv.at[step, source],
-                device_id={"tm": source},
-                device_id_type=MESH,
-            ).wait_recv()
-        return carry
-
-    lax.fori_loop(0, count - 1, arrived, 0)
-
-    row_tiles = slab // 8
+            arrival(step, lax.rem(t + k, count)).wait_recv()
+        return carry
+
+    lax.fori_loop(1, count, arrived, 0)
+
+    @pl.when(home != c)
+    def _():
+        for step in (0, 1):
+            arrival(step, t).wait_recv()
+
+    row_tiles = piece // 8
 
     def transform(p, carry):
         r = pl.multiple_of((p // tiles) * 8, 8)
         q = pl.multiple_of(lax.rem(p, tiles) * 128, 128)
         x = [by_cell[n, pl.ds(r, 8), pl.ds(q, 128)] for n in range(length)]
         f = rfft_list(x)
-        here = (pl.ds(pl.multiple_of(r + 8, 8), 8), pl.ds(q, 128))
-        spec[(0,) + here] = f[0][0]
-        spec[(1,) + here] = f[pairs][0]
+        here = (pl.ds(pl.multiple_of(r + 8 + piece * c, 8), 8), pl.ds(q, 128))
+        spec[(0, 0) + here] = f[0][0]
+        spec[(0, 1) + here] = f[pairs][0]
         for j in range(1, pairs):
-            spec[(2 * j,) + here] = f[j][0]
-            spec[(2 * j + 1,) + here] = f[j][1]
+            for part in (0, 1):
+                spec[(j // share, 2 * (j % share) + part) + here] = f[j][part]
         return carry
 
     lax.fori_loop(0, row_tiles * tiles, transform, 0)
 
-    north, south = pos(lax.rem(me + total - 1, total)), pos(lax.rem(me + 1, total))
-
-    def halo(side, q):
+    beyond = {"tm": lax.rem(t + count + 2 * c - 1, count)}
+    src_edge = pl.ds(pl.multiple_of(8 + (slab - 8) * c, 8), 8)
+    dst_edge = pl.ds(pl.multiple_of((slab + 8) * (1 - c), 8), 8)
+
+    def halo(group, q):
         fields = pl.ds(2 * q, 2)
-        if side == 0:
-            src, dst, target = slab, 0, south
-        else:
-            src, dst, target = 8, slab + 8, north
         return pltpu.make_async_remote_copy(
-            src_ref=spec.at[fields, pl.ds(src, 8)],
-            dst_ref=spec.at[fields, pl.ds(dst, 8)],
-            send_sem=h_send.at[side, q],
-            recv_sem=h_recv.at[side, q],
-            device_id=target,
+            src_ref=spec.at[group, fields, src_edge],
+            dst_ref=spec.at[group, fields, dst_edge],
+            send_sem=h_send.at[group, q],
+            recv_sem=h_recv.at[1 - c, q],
+            device_id={**beyond, "rows": group},
+            device_id_type=MESH,
+        )
+
+    own_part = pl.ds(pl.multiple_of(8 + piece * c, 8), piece)
+
+    def swap(q):
+        fields = pl.ds(2 * q, 2)
+        return pltpu.make_async_remote_copy(
+            src_ref=spec.at[1 - c, fields, own_part],
+            dst_ref=spec.at[1 - c, fields, own_part],
+            send_sem=x_send.at[q],
+            recv_sem=x_recv.at[q],
+            device_id=partner,
             device_id_type=MESH,
         )
 
     def send_halo(q, carry):
         halo(0, q).start()
         halo(1, q).start()
-        return carry
-
-    lax.fori_loop(0, pairs, send_halo, 0)
-
-    top = jnp.where(me == 0, 0.0, 1.0)
-    bottom = jnp.where(me == total - 1, 0.0, 1.0)
-    n_tr = row_tiles + 2
+        swap(q).start()
+        return carry
+
+    lax.fori_loop(0, share, send_halo, 0)
+
+    top = jnp.where(t == 0, 0.0, 1.0)
+    bottom = jnp.where(t == count - 1, 0.0, 1.0)
+    n_tr = slab // 8 + 2
     sub = lax.broadcasted_iota(jnp.int32, (8, cols), 0)
 
-    def spread_of(v, wanted):
+    def spread_of(v, wanted, shift):
         down = [pltpu.roll(x, 1, 0) for x in v]
         up = [pltpu.roll(x, 7, 0) for x in v]
         out = {}
@@ -471,7 +513,7 @@
             v_s = jnp.where(sub == 7, up[min(i + 1, n_tr - 1)], up[i])
             here = slice(8 * i, 8 * i + 8)
             out[i] = (
-                weights[0, here, :] * v[i]
+                (weights[0, here, :] + shift) * v[i]
                 - weights[1, here, :] * v_n
                 - weights[2, here, :] * v_s
                 - weights[3, here, :] * pltpu.roll(v[i], 1, 1)
@@ -498,21 +540,37 @@
         return jnp.sum(acc, axis=0, keepdims=True)
 
     def solve(q, carry):
-        halo(0, q).wait_recv()
-        halo(1, q).wait_recv()
-        a_re, a_im, b = tab[2 * length + q], tab[2 * length + pairs + q], tab[2 * length + 2 * pairs + q]
+        for side in (0, 1):
+            pltpu.make_async_remote_copy(
+                src_ref=spec.at[c, pl.ds(2 * q, 2), src_edge],
+                dst_ref=spec.at[c, pl.ds(2 * q, 2), pl.ds((slab + 8) * side, 8)],
+                send_sem=h_send.at[0, q],
+                recv_sem=h_recv.at[side, q],
+                device_id=partner,
+                device_id_type=MESH,
+            ).wait_recv()
+        pltpu.make_async_remote_copy(
+            src_ref=spec.at[c, pl.ds(2 * q, 2), own_part],
+            dst_ref=spec.at[c, pl.ds(2 * q, 2), pl.ds(pl.multiple_of(8 + piece * (1 - c), 8), piece)],
+            send_sem=x_send.at[q],
+            recv_sem=x_recv.at[q],
+            device_id=partner,
+            device_id_type=MESH,
+        ).wait_recv()
+        j = 2 * length + share * c + q
+        a_re, a_im, b = tab[j], tab[j + pairs], tab[j + 2 * pairs]
         v = [
-            [clip(i, spec[2 * q + part, 8 * i : 8 * i + 8, :]) for i in range(n_tr)]
+            [clip(i, spec[c, 2 * q + part, 8 * i : 8 * i + 8, :]) for i in range(n_tr)]
             for part in (0, 1)
         ]
         for order in range(6):
             wanted = inner if order == 5 else range(n_tr)
             sign = b if order % 2 == 0 else -b
-            k_re, k_im = spread_of(v[0], wanted), spread_of(v[1], wanted)
+            k_re, k_im = spread_of(v[0], wanted, a_re), spread_of(v[1], wanted, a_im)
             new_re, new_im = [None] * n_tr, [None] * n_tr
             for i in wanted:
-                new_re[i] = clip(i, a_re * v[0][i] + sign * v[1][i] + k_re[i])
-                new_im[i] = clip(i, a_im * v[1][i] - sign * v[0][i] + k_im[i])
+                new_re[i] = sign * v[1][i] + k_re[i]
+                new_im[i] = k_im[i] - sign * v[0][i]
             v = [new_re, new_im]
             mom[2 * order, pl.ds(q, 1), :] = folded(v[0])
             mom[2 * order + 1, pl.ds(q, 1), :] = folded(v[1])
@@ -523,61 +581,60 @@
                         keep[2 * q + part, 8 * i - 8 : 8 * i, :] = v[part][i]
         return carry
 
-    lax.fori_loop(0, pairs, solve, 0)
-
-    row = lax.broadcasted_iota(jnp.int32, (pairs, 128), 0)
+    lax.fori_loop(0, share, solve, 0)
+
     lane8 = lax.broadcasted_iota(jnp.int32, (8, 128), 1)
     row8 = lax.broadcasted_iota(jnp.int32, (8, 128), 0)
+    apart = (row8 == 0) & (c == 0)
     packed = [jnp.zeros((8, 128), jnp.float32), jnp.zeros((8, 128), jnp.float32)]
 
     def slot(k, g):
-        return lane8 == (16 * row8 + 2 * k + g if g < 2 else 16 * k + 12)
+        return lane8 == (16 * row8 + k if g == 0 else 16 * k + 12)
 
     for k in range(6):
         re, im = mom[2 * k], mom[2 * k + 1]
-        both = jnp.where(row == 0, re, re + im)
-        for g in range(3):
-            x = both[8 * g : 8 * g + 8] if g < 2 else im[0:8]
+        both = jnp.where(apart, re, re + im)
+        for g, x in enumerate((both, im)):
             big = 256.0 * jnp.max(x, axis=1, keepdims=True)
             hi = (x + big) - big
             lo = x - hi
-            where = slot(k, g) if g < 2 else slot(k, g) & (row8 == 0)
+            where = slot(k, g) if g == 0 else slot(k, g) & (row8 == 0)
             packed[0] = jnp.where(where, jnp.sum(hi, axis=1, keepdims=True), packed[0])
             packed[1] = jnp.where(where, jnp.sum(lo, axis=1, keepdims=True), packed[1])
     mine = jnp.concatenate([jnp.sum(x, axis=0, keepdims=True) for x in packed], axis=1)
     ar_send[...] = mine
-    ar_all[me] = mine
-
-    def share(k):
+    ar_all[t] = mine
+
+    def tell(k):
         return pltpu.make_async_remote_copy(
             src_ref=ar_send,
-            dst_ref=ar_all.at[me],
+            dst_ref=ar_all.at[t],
             send_sem=m_send.at[k],
-            recv_sem=m_recv.at[me],
-            device_id=pos(lax.rem(me + k, total)),
+            recv_sem=m_recv.at[t],
+            device_id={"tm": lax.rem(t + k, count)},
             device_id_type=MESH,
         )
 
-    def share_one(k, carry):
-        share(k).start()
-        return carry
-
-    lax.fori_loop(1, total, share_one, 0)
-
-    def shared(k, carry):
-        source = lax.rem(me + k, total)
+    def tell_one(k, carry):
+        tell(k).start()
+        return carry
+
+    lax.fori_loop(1, count, tell_one, 0)
+
+    def told(k, carry):
+        source = lax.rem(t + k, count)
         pltpu.make_async_remote_copy(
             src_ref=ar_send,
             dst_ref=ar_all.at[source],
             send_sem=m_send.at[k],
             recv_sem=m_recv.at[source],
-            device_id=pos(source),
+            device_id={"tm": source},
             device_id_type=MESH,
         ).wait_recv()
         return carry
 
-    lax.fori_loop(1, total, shared, 0)
-    sums = [(ar_all[i][:, 0:128], ar_all[i][:, 128:256]) for i in range(total)]
+    lax.fori_loop(1, count, told, 0)
+    sums = [(ar_all[i][:, 0:128], ar_all[i][:, 128:256]) for i in range(count)]
     while len(sums) > 1:
         sums = [pair_add(sums[2 * i], sums[2 * i + 1]) for i in range(len(sums) // 2)]
     whole = [jnp.broadcast_to(x, (8, 128)) for x in sums[0]]
@@ -589,49 +646,93 @@
                 jnp.broadcast_to(
                     jnp.sum(jnp.where(slot(k, g), x, 0.0), axis=1, keepdims=True), (8, 128)
                 )
-                for g in range(3)
+                for g in range(2)
             ]
             sides.append(jnp.concatenate(groups, axis=0))
         mu.append(tuple(sides))
     for k, w in enumerate(krylov_weights(mu)):
-        coef[k, 0] = w[0:pairs]
-        coef[k, 1] = jnp.where(row == 0, w[pairs : pairs + 1], w[0:pairs])
+        coef[k, 0] = w[0:share]
+        coef[k, 1] = jnp.where(apart, w[share : share + 1], w[0:share])
+
+    def blend(q, part_rows):
+        for part in (0, 1):
+            f = 2 * q + part
+            total = None
+            for k, ref in enumerate((v0_ref, v1_ref, v2_ref)):
+                w = jnp.concatenate([coef[k, part, pl.ds(q, 1), :]] * tiles, axis=1)
+                term = w * ref[f, part_rows, :]
+                total = term if total is None else total + term
+            xs[c, f, part_rows, :] = total
+
+    my_rows = pl.ds(pl.multiple_of(piece * c, piece), piece)
+    other_rows = pl.ds(pl.multiple_of(piece * (1 - c), piece), piece)
+
+    def give(q, part_rows, group):
+        block = xs.at[group, pl.ds(2 * q, 2), part_rows]
+        return pltpu.make_async_remote_copy(
+            src_ref=block,
+            dst_ref=block,
+            send_sem=y_send.at[q],
+            recv_sem=y_recv.at[q],
+            device_id=partner,
+            device_id_type=MESH,
+        )
+
+    def blend_other(q, carry):
+        blend(q, other_rows)
+        give(q, other_rows, c).start()
+        return carry
+
+    lax.fori_loop(0, share, blend_other, 0)
+
+    def blend_own(q, carry):
+        blend(q, my_rows)
+        return carry
+
+    lax.fori_loop(0, share, blend_own, 0)
+
+    def given(q, carry):
+        give(q, my_rows, 1 - c).wait_recv()
+        return carry
+
+    lax.fori_loop(0, share, given, 0)
 
     def restore(p, carry):
         r = pl.multiple_of((p // tiles) * 8, 8)
         q = pl.multiple_of(lax.rem(p, tiles) * 128, 128)
-        here = (pl.ds(r, 8), pl.ds(q, 128))
-
-        def field(f):
-            j, part = f // 2, f % 2
-            out = coef[0, part, j : j + 1, :] * v0_ref[(f,) + here]
-            out = out + coef[1, part, j : j + 1, :] * v1_ref[(f,) + here]
-            return out + coef[2, part, j : j + 1, :] * v2_ref[(f,) + here]
-
-        freq = [(field(0), None)]
-        freq += [(field(2 * j), field(2 * j + 1)) for j in range(1, pairs)]
-        freq += [(field(1), None)]
+        here = (pl.ds(pl.multiple_of(r + piece * c, 8), 8), pl.ds(q, 128))
+        freq = [(xs[(0, 0) + here], None)]
+        for j in range(1, pairs):
+            freq.append(tuple(xs[(j // share, 2 * (j % share) + part) + here] for part in (0, 1)))
+        freq.append((xs[(0, 1) + here], None))
         for n, x in enumerate(irfft_list(freq)):
-            corr[(n,) + here] = x * tab[length + n]
+            corr[n, pl.ds(r, 8), pl.ds(q, 128)] = x * tab[length + n]
         return carry
 
     lax.fori_loop(0, row_tiles * tiles, restore, 0)
 
-    own = pl.ds(pl.multiple_of(t * slab, slab), slab)
+    def block_of(source, core):
+        return pl.multiple_of(lax.rem(source, half) * slab + piece * core, 8)
+
+    def returning(dest):
+        return pltpu.make_async_remote_copy(
+            src_ref=corr.at[pl.ds(2 * dest, 2)],
+            dst_ref=back.at[:, pl.ds(block_of(t, c), piece)],
+            send_sem=b_send.at[dest],
+            recv_sem=b_recv.at[place, c],
+            device_id={"tm": dest, "rows": home},
+            device_id_type=MESH,
+        )
 
     def send_back(k, carry):
-        dest = peer(k)
-        pltpu.make_async_remote_copy(
-            src_ref=corr.at[pl.ds(2 * dest, 2)],
-            dst_ref=back.at[:, own],
-            send_sem=b_send.at[k],
-            recv_sem=b_recv.at[t],
-            device_id={"tm": dest},
-            device_id_type=MESH,
-        ).start()
+        returning(peer(k)).start()
         return carry
 
     lax.fori_loop(0, count - 1, send_back, 0)
+
+    @pl.when(home != c)
+    def _():
+        returning(t).start()
 
     sq_copy.wait()
     rms = jnp.sqrt(
@@ -640,28 +741,35 @@
     )
     rms_ref[...] = jnp.broadcast_to(rms[:, 0], (2, 128))
 
-    def final(source, piece):
-        block = pl.ds(pl.multiple_of(source * slab, slab), slab)
-        ahead = pl.ds(pl.multiple_of(source * slab + 8, 8), slab)
-        out_ref[:, block, :] = u_ext[:, ahead, :] + piece
-
-    final(t, corr[pl.ds(2 * t, 2)])
-
-    def returned(k, carry):
-        source = peer(k)
-        block = pl.ds(pl.multiple_of(source * slab, slab), slab)
-        pltpu.make_async_remote_copy(
-            src_ref=corr.at[pl.ds(0, 2)],
-            dst_ref=back.at[:, block],
-            send_sem=b_send.at[k],
-            recv_sem=b_recv.at[source],
-            device_id={"tm": source},
-            device_id_type=MESH,
-        ).wait_recv()
-        final(source, back[:, block, :])
-        return carry
-
-    lax.fori_loop(0, count - 1, returned, 0)
+    def final(source, core, piece_of):
+        start = block_of(source, core)
+        ahead = pl.ds(pl.multiple_of(start + 8, 8), piece)
+        out_ref[:, pl.ds(start, piece), :] = u_ext[:, ahead, :] + piece_of
+
+    @pl.when(home == c)
+    def _():
+        final(t, c, corr[pl.ds(2 * t, 2)])
+
+    def returned(j, carry):
+        source = chip(j)
+        for core in (0, 1):
+
+            @pl.when(elsewhere(source, core))
+            def _():
+                block = pl.ds(block_of(source, core), piece)
+                pltpu.make_async_remote_copy(
+                    src_ref=corr.at[pl.ds(0, 2)],
+                    dst_ref=back.at[:, block],
+                    send_sem=b_send.at[0],
+                    recv_sem=b_recv.at[lax.rem(source, half), core],
+                    device_id={"tm": source},
+                    device_id_type=MESH,
+                ).wait_recv()
+                final(source, core, back[:, block, :])
+
+        return carry
+
+    lax.fori_loop(0, half, returned, 0)
 
     for rim in rims:
         rim.wait_send()
@@ -670,33 +778,43 @@
     def _():
         onward.wait_send()
 
-    def drain_peers(k, carry):
-        forward(0, peer(k)).wait_send()
-        forward(1, peer(k)).wait_send()
-        pltpu.make_async_remote_copy(
-            src_ref=corr.at[pl.ds(0, 2)],
-            dst_ref=back.at[:, own],
-            send_sem=b_send.at[k],
-            recv_sem=b_recv.at[t],
-            device_id={"tm": peer(k)},
-            device_id_type=MESH,
-        ).wait_send()
-        return carry
-
-    lax.fori_loop(0, count - 1, drain_peers, 0)
-
-    def drain_halo(q, carry):
+    def drain_forward(j, carry):
+        dest = chip(j)
+        for core in (0, 1):
+
+            @pl.when(elsewhere(dest, core))
+            def _():
+                forward(0, dest, core).wait_send()
+                forward(1, dest, core).wait_send()
+
+        return carry
+
+    lax.fori_loop(0, half, drain_forward, 0)
+
+    def drain_back(k, carry):
+        returning(peer(k)).wait_send()
+        return carry
+
+    lax.fori_loop(0, count - 1, drain_back, 0)
+
+    @pl.when(home != c)
+    def _():
+        returning(t).wait_send()
+
+    def drain_pairs(q, carry):
         halo(0, q).wait_send()
         halo(1, q).wait_send()
-        return carry
-
-    lax.fori_loop(0, pairs, drain_halo, 0)
-
-    def drain_share(k, carry):
-        share(k).wait_send()
-        return carry
-
-    lax.fori_loop(1, total, drain_share, 0)
+        swap(q).wait_send()
+        give(q, other_rows, c).wait_send()
+        return carry
+
+    lax.fori_loop(0, share, drain_pairs, 0)
+
+    def drain_tell(k, carry):
+        tell(k).wait_send()
+        return carry
+
+    lax.fori_loop(1, count, drain_tell, 0)
 
 
 def tables(length):
@@ -718,9 +836,9 @@
     halves = lax.axis_size("rows")
     length = steps * count
     assert steps == 2 and halves == 2
-    slab = rows // count
+    slab = 2 * rows // count
     pairs = length // 2
-    total = 2 * count
+    share = pairs // 2
     cells = rows * halves * cols
     f32 = jnp.float32
     vmem = pltpu.VMEM
@@ -738,34 +856,39 @@
             vmem((steps, rows + 16, cols), f32),
             vmem((steps, rows, cols), f32),
             vmem((rows, cols), f32),
-            vmem((rows + 32, cols), f32),
+            vmem((2 * rows + 32, cols), f32),
             vmem((steps, rows, cols), f32),
-            vmem((length, slab, cols), f32),
-            vmem((length, slab + 16, cols), f32),
-            vmem((length, slab, cols), f32),
-            vmem((length, slab, cols), f32),
-            vmem((length, slab, cols), f32),
-            vmem((length, slab, cols), f32),
+            vmem((length, slab // 2, cols), f32),
+            vmem((2, pairs, slab + 16, cols), f32),
+            vmem((pairs, slab, cols), f32),
+            vmem((pairs, slab, cols), f32),
+            vmem((pairs, slab, cols), f32),
+            vmem((2, pairs, slab, cols), f32),
+            vmem((length, slab // 2, cols), f32),
             vmem((steps, rows, cols), f32),
             vmem((5, slab + 16, cols), f32),
-            vmem((12, pairs, 128), f32),
-            vmem((3, 2, pairs, 128), f32),
+            vmem((12, share, 128), f32),
+            vmem((3, 2, share, 128), f32),
             vmem((1, 256), f32),
-            vmem((total, 1, 256), f32),
+            vmem((count, 1, 256), f32),
             vmem((2, 8, 128), f32),
             vmem((2, 8, 128), f32),
             dma((3,)),
             dma((3,)),
             dma((3,)),
             dma((3,)),
+            dma((2, count // 2, 2)),
             dma((2, count)),
-            dma((2, count)),
-            dma((2, pairs)),
-            dma((2, pairs)),
-            dma((total,)),
-            dma((total,)),
+            dma((2, share)),
+            dma((2, share)),
+            dma((share,)),
+            dma((share,)),
+            dma((share,)),
+            dma((share,)),
             dma((count,)),
             dma((count,)),
+            dma((count,)),
+            dma((count // 2, 2)),
             pltpu.SemaphoreType.REGULAR,
             pltpu.SemaphoreType.REGULAR,
         ],

time: 149 us -> 144 us (0.966)
  Pallas kernels: 147 us -> 142 us
    pallas_call x1, Pallas kernels: 147 us -> 142 us  [shards(): pl.pallas_call(functools.partial(kernel, count, cells), out_shape=(vmem((...]
where the time goes in v3:
time: 144 us
  Pallas kernels  142 us (99%)
  local copies, waits for them, and re-layouts  1.6 us (1%)
    pallas_call x1, Pallas kernels, shards(): pl.pallas_call(functools.partial(kernel, count, cells), out_shape=(vmem((...  142 us

profile of v3, /device:TPU:69, one launch (start us, length us, event | category | flops | bytes accessed | tf_op | source)
XLA Modules:
  0.0 143.8 jit_solution(12819003438131029679)
XLA Ops:
  0.6 141.5 %paradiag.1 = (f32[2,256,512]{2,1,0:T(8,128)S(1)}, f32[2,128]{1,0:T(2,128)S(1)}) custom-call(f32[2,256,512]{2,1,0:T(8,128)} %it_hbm.1, f32[2,256,512]{2,1,0:T(8,128)} %fo_hbm.1, f32[256,512]{1,0:T(8,128)} %init_hbm.1, f32[256,512]{1,0:T(8,128)} %di_hbm.1, f32[112]{0:T(128)} %constant.2.clone.tab), custom_call_target="tpu_custom_call" | custom-call | tf_op jit(solution)/shard_map/paradiag/pallas_call | solution.py:847
  142.2 1.0 copy.8
  143.1 0.6 slice_reduce_fusion

commit v4 on v3

--- a/solution.py
+++ b/solution.py
@@ -172,14 +172,13 @@
     d_ext,
     res,
     by_cell,
+    stop,
     spec,
-    v0_ref,
-    v1_ref,
-    v2_ref,
-    xs,
+    basis,
     corr,
     back,
     weights,
+    lined,
     mom,
     coef,
     ar_send,
@@ -188,6 +187,7 @@
     sq_recv,
     load_sem,
     prev_sem,
+    hop_sem,
     rim_send,
     rim_recv,
     a_send,
@@ -207,6 +207,8 @@
 ):
     t = lax.axis_index("tm")
     c = lax.axis_index("rows")
+    me = c * count + t
+    total = 2 * count
     length = 2 * count
     pairs = length // 2
     share = pairs // 2
@@ -218,6 +220,9 @@
     tiles = cols // 128
     home = t // half
     place = lax.rem(t, half)
+
+    def pos(i):
+        return {"tm": lax.rem(i, count), "rows": i // count}
 
     barrier = pltpu.get_barrier_semaphore()
 
@@ -364,22 +369,54 @@
             by_cell[2 * t + step] = res[step, pl.ds(start, piece), :]
             forward(step, t, 1 - c).start()
 
+    across = lax.rem(t + half, count)
+    hop = pltpu.make_async_remote_copy(
+        src_ref=res.at[1, pl.ds(pl.multiple_of(lax.rem(across, half) * slab, slab), slab)],
+        dst_ref=stop,
+        send_sem=hop_sem.at[0],
+        recv_sem=hop_sem.at[1],
+        device_id={"tm": lax.rem(t + count - half // 2, count)},
+        device_id_type=MESH,
+    )
+    origin = lax.rem(t + half // 2, count)
+    relays = lax.rem(origin + half, count) // half == c
+
+    def hop_on(core):
+        return pltpu.make_async_remote_copy(
+            src_ref=stop.at[pl.ds(piece * core, piece)],
+            dst_ref=by_cell.at[2 * origin + 1],
+            send_sem=hop_sem.at[2 + core],
+            recv_sem=a_recv.at[1, origin],
+            device_id={"tm": lax.rem(t + count - half // 2, count), "rows": core},
+            device_id_type=MESH,
+        )
+
     def widen(k, carry):
         pl.semaphore_signal(from_left, inc=1, device_id=right, device_id_type=MESH)
         pl.semaphore_signal(from_right, inc=1, device_id=left, device_id_type=MESH)
         pl.semaphore_wait(from_left, 1)
         pl.semaphore_wait(from_right, 1)
-        send_one(1, lax.rem(t + k, count))
-
         @pl.when(k < half)
         def _():
+            send_one(1, lax.rem(t + k, count))
             send_one(1, lax.rem(t + count - k, count))
+
+        @pl.when((k == half // 2) & (home != c))
+        def _():
+            make(1, across)
+            hop.start()
 
         return carry
 
     sq_send[...] = jnp.zeros((2, 8, 128), jnp.float32)
     lax.fori_loop(1, half + 1, widen, 0)
     send_home(1)
+
+    @pl.when(relays)
+    def _():
+        hop.wait_recv()
+        hop_on(0).start()
+        hop_on(1).start()
 
     @pl.when(t > 0)
     def _():
@@ -502,15 +539,19 @@
     top = jnp.where(t == 0, 0.0, 1.0)
     bottom = jnp.where(t == count - 1, 0.0, 1.0)
     n_tr = slab // 8 + 2
-    sub = lax.broadcasted_iota(jnp.int32, (8, cols), 0)
-
-    def spread_of(v, wanted, shift):
-        down = [pltpu.roll(x, 1, 0) for x in v]
-        up = [pltpu.roll(x, 7, 0) for x in v]
+
+    def spread_of(v, wanted, shift, part):
+        for i in range(n_tr):
+            for k in range(tiles):
+                lined[part, k, 8 * i + 8 : 8 * i + 16, :] = v[i][:, 128 * k : 128 * k + 128]
         out = {}
         for i in wanted:
-            v_n = jnp.where(sub == 0, down[max(i - 1, 0)], down[i])
-            v_s = jnp.where(sub == 7, up[min(i + 1, n_tr - 1)], up[i])
+            v_n, v_s = (
+                jnp.concatenate(
+                    [lined[part, k, 8 * i + 8 + o : 8 * i + 16 + o, :] for k in range(tiles)], axis=1
+                )
+                for o in (-1, 1)
+            )
             here = slice(8 * i, 8 * i + 8)
             out[i] = (
                 (weights[0, here, :] + shift) * v[i]
@@ -538,6 +579,16 @@
                 part = sq[:, 128 * k : 128 * k + 128]
                 acc = part if acc is None else acc + part
         return jnp.sum(acc, axis=0, keepdims=True)
+
+    def give(q):
+        return pltpu.make_async_remote_copy(
+            src_ref=basis.at[2, :, pl.ds(2 * q, 2)],
+            dst_ref=basis.at[c, :, pl.ds(2 * q, 2)],
+            send_sem=y_send.at[q],
+            recv_sem=y_recv.at[q],
+            device_id=partner,
+            device_id_type=MESH,
+        )
 
     def solve(q, carry):
         for side in (0, 1):
@@ -566,7 +617,7 @@
         for order in range(6):
             wanted = inner if order == 5 else range(n_tr)
             sign = b if order % 2 == 0 else -b
-            k_re, k_im = spread_of(v[0], wanted, a_re), spread_of(v[1], wanted, a_im)
+            k_re, k_im = spread_of(v[0], wanted, a_re, 0), spread_of(v[1], wanted, a_im, 1)
             new_re, new_im = [None] * n_tr, [None] * n_tr
             for i in wanted:
                 new_re[i] = sign * v[1][i] + k_re[i]
@@ -575,43 +626,47 @@
             mom[2 * order, pl.ds(q, 1), :] = folded(v[0])
             mom[2 * order + 1, pl.ds(q, 1), :] = folded(v[1])
             if order % 2 == 0:
-                keep = (v0_ref, v1_ref, v2_ref)[order // 2]
                 for part in (0, 1):
                     for i in inner:
-                        keep[2 * q + part, 8 * i - 8 : 8 * i, :] = v[part][i]
-        return carry
-
+                        line = (8 * i - 8) % piece
+                        keep = 2 * c if 8 * i - 8 < piece else 2 - c
+                        basis[keep, order // 2, 2 * q + part, line : line + 8, :] = v[part][i]
+        give(q).start()
+        return carry
+
+    lined[...] = jnp.zeros(lined.shape, jnp.float32)
     lax.fori_loop(0, share, solve, 0)
 
     lane8 = lax.broadcasted_iota(jnp.int32, (8, 128), 1)
     row8 = lax.broadcasted_iota(jnp.int32, (8, 128), 0)
+    row16 = lax.broadcasted_iota(jnp.int32, (pairs, 128), 0)
     apart = (row8 == 0) & (c == 0)
     packed = [jnp.zeros((8, 128), jnp.float32), jnp.zeros((8, 128), jnp.float32)]
 
     def slot(k, g):
-        return lane8 == (16 * row8 + k if g == 0 else 16 * k + 12)
+        return lane8 == (16 * row8 + 2 * k + g if g is not None else 16 * k + 12)
 
     for k in range(6):
         re, im = mom[2 * k], mom[2 * k + 1]
         both = jnp.where(apart, re, re + im)
-        for g, x in enumerate((both, im)):
+        for g, x in ((c, both), (None, im)):
             big = 256.0 * jnp.max(x, axis=1, keepdims=True)
             hi = (x + big) - big
             lo = x - hi
-            where = slot(k, g) if g == 0 else slot(k, g) & (row8 == 0)
+            where = slot(k, g) if g is not None else slot(k, g) & apart
             packed[0] = jnp.where(where, jnp.sum(hi, axis=1, keepdims=True), packed[0])
             packed[1] = jnp.where(where, jnp.sum(lo, axis=1, keepdims=True), packed[1])
     mine = jnp.concatenate([jnp.sum(x, axis=0, keepdims=True) for x in packed], axis=1)
     ar_send[...] = mine
-    ar_all[t] = mine
+    ar_all[me] = mine
 
     def tell(k):
         return pltpu.make_async_remote_copy(
             src_ref=ar_send,
-            dst_ref=ar_all.at[t],
+            dst_ref=ar_all.at[me],
             send_sem=m_send.at[k],
-            recv_sem=m_recv.at[t],
-            device_id={"tm": lax.rem(t + k, count)},
+            recv_sem=m_recv.at[me],
+            device_id=pos(lax.rem(me + k, total)),
             device_id_type=MESH,
         )
 
@@ -619,22 +674,22 @@
         tell(k).start()
         return carry
 
-    lax.fori_loop(1, count, tell_one, 0)
+    lax.fori_loop(1, total, tell_one, 0)
 
     def told(k, carry):
-        source = lax.rem(t + k, count)
+        source = lax.rem(me + k, total)
         pltpu.make_async_remote_copy(
             src_ref=ar_send,
             dst_ref=ar_all.at[source],
             send_sem=m_send.at[k],
             recv_sem=m_recv.at[source],
-            device_id={"tm": source},
+            device_id=pos(source),
             device_id_type=MESH,
         ).wait_recv()
         return carry
 
-    lax.fori_loop(1, count, told, 0)
-    sums = [(ar_all[i][:, 0:128], ar_all[i][:, 128:256]) for i in range(count)]
+    lax.fori_loop(1, total, told, 0)
+    sums = [(ar_all[i][:, 0:128], ar_all[i][:, 128:256]) for i in range(total)]
     while len(sums) > 1:
         sums = [pair_add(sums[2 * i], sums[2 * i + 1]) for i in range(len(sums) // 2)]
     whole = [jnp.broadcast_to(x, (8, 128)) for x in sums[0]]
@@ -646,53 +701,23 @@
                 jnp.broadcast_to(
                     jnp.sum(jnp.where(slot(k, g), x, 0.0), axis=1, keepdims=True), (8, 128)
                 )
-                for g in range(2)
+                for g in (0, 1, None)
             ]
             sides.append(jnp.concatenate(groups, axis=0))
         mu.append(tuple(sides))
     for k, w in enumerate(krylov_weights(mu)):
-        coef[k, 0] = w[0:share]
-        coef[k, 1] = jnp.where(apart, w[share : share + 1], w[0:share])
-
-    def blend(q, part_rows):
-        for part in (0, 1):
-            f = 2 * q + part
-            total = None
-            for k, ref in enumerate((v0_ref, v1_ref, v2_ref)):
-                w = jnp.concatenate([coef[k, part, pl.ds(q, 1), :]] * tiles, axis=1)
-                term = w * ref[f, part_rows, :]
-                total = term if total is None else total + term
-            xs[c, f, part_rows, :] = total
-
-    my_rows = pl.ds(pl.multiple_of(piece * c, piece), piece)
-    other_rows = pl.ds(pl.multiple_of(piece * (1 - c), piece), piece)
-
-    def give(q, part_rows, group):
-        block = xs.at[group, pl.ds(2 * q, 2), part_rows]
-        return pltpu.make_async_remote_copy(
-            src_ref=block,
-            dst_ref=block,
+        coef[k, 0] = w[0:pairs]
+        coef[k, 1] = jnp.where(row16 == 0, w[pairs : pairs + 1], w[0:pairs])
+
+    def given(q, carry):
+        pltpu.make_async_remote_copy(
+            src_ref=basis.at[2, :, pl.ds(2 * q, 2)],
+            dst_ref=basis.at[1 - c, :, pl.ds(2 * q, 2)],
             send_sem=y_send.at[q],
             recv_sem=y_recv.at[q],
             device_id=partner,
             device_id_type=MESH,
-        )
-
-    def blend_other(q, carry):
-        blend(q, other_rows)
-        give(q, other_rows, c).start()
-        return carry
-
-    lax.fori_loop(0, share, blend_other, 0)
-
-    def blend_own(q, carry):
-        blend(q, my_rows)
-        return carry
-
-    lax.fori_loop(0, share, blend_own, 0)
-
-    def given(q, carry):
-        give(q, my_rows, 1 - c).wait_recv()
+        ).wait_recv()
         return carry
 
     lax.fori_loop(0, share, given, 0)
@@ -700,11 +725,18 @@
     def restore(p, carry):
         r = pl.multiple_of((p // tiles) * 8, 8)
         q = pl.multiple_of(lax.rem(p, tiles) * 128, 128)
-        here = (pl.ds(pl.multiple_of(r + piece * c, 8), 8), pl.ds(q, 128))
-        freq = [(xs[(0, 0) + here], None)]
-        for j in range(1, pairs):
-            freq.append(tuple(xs[(j // share, 2 * (j % share) + part) + here] for part in (0, 1)))
-        freq.append((xs[(0, 1) + here], None))
+        here = (pl.ds(r, 8), pl.ds(q, 128))
+
+        def field(j, part):
+            terms = [
+                coef[k, part, j : j + 1, :] * basis[(j // share, k, 2 * (j % share) + part) + here]
+                for k in range(3)
+            ]
+            return terms[0] + terms[1] + terms[2]
+
+        freq = [(field(0, 0), None)]
+        freq += [(field(j, 0), field(j, 1)) for j in range(1, pairs)]
+        freq += [(field(0, 1), None)]
         for n, x in enumerate(irfft_list(freq)):
             corr[n, pl.ds(r, 8), pl.ds(q, 128)] = x * tab[length + n]
         return carry
@@ -785,11 +817,23 @@
             @pl.when(elsewhere(dest, core))
             def _():
                 forward(0, dest, core).wait_send()
+
+            @pl.when(elsewhere(dest, core) & (dest != across))
+            def _():
                 forward(1, dest, core).wait_send()
 
         return carry
 
     lax.fori_loop(0, half, drain_forward, 0)
+
+    @pl.when(home != c)
+    def _():
+        hop.wait_send()
+
+    @pl.when(relays)
+    def _():
+        hop_on(0).wait_send()
+        hop_on(1).wait_send()
 
     def drain_back(k, carry):
         returning(peer(k)).wait_send()
@@ -805,7 +849,7 @@
         halo(0, q).wait_send()
         halo(1, q).wait_send()
         swap(q).wait_send()
-        give(q, other_rows, c).wait_send()
+        give(q).wait_send()
         return carry
 
     lax.fori_loop(0, share, drain_pairs, 0)
@@ -814,7 +858,7 @@
         tell(k).wait_send()
         return carry
 
-    lax.fori_loop(1, count, drain_tell, 0)
+    lax.fori_loop(1, total, drain_tell, 0)
 
 
 def tables(length):
@@ -859,22 +903,22 @@
             vmem((2 * rows + 32, cols), f32),
             vmem((steps, rows, cols), f32),
             vmem((length, slab // 2, cols), f32),
+            vmem((slab, cols), f32),
             vmem((2, pairs, slab + 16, cols), f32),
-            vmem((pairs, slab, cols), f32),
-            vmem((pairs, slab, cols), f32),
-            vmem((pairs, slab, cols), f32),
-            vmem((2, pairs, slab, cols), f32),
+            vmem((3, 3, pairs, slab // 2, cols), f32),
             vmem((length, slab // 2, cols), f32),
             vmem((steps, rows, cols), f32),
             vmem((5, slab + 16, cols), f32),
+            vmem((2, cols // 128, slab + 32, 128), f32),
             vmem((12, share, 128), f32),
-            vmem((3, 2, share, 128), f32),
+            vmem((3, 2, pairs, 128), f32),
             vmem((1, 256), f32),
-            vmem((count, 1, 256), f32),
+            vmem((2 * count, 1, 256), f32),
             vmem((2, 8, 128), f32),
             vmem((2, 8, 128), f32),
             dma((3,)),
             dma((3,)),
+            dma((4,)),
             dma((3,)),
             dma((3,)),
             dma((2, count // 2, 2)),
@@ -885,8 +929,8 @@
             dma((share,)),
             dma((share,)),
             dma((share,)),
-            dma((count,)),
-            dma((count,)),
+            dma((2 * count,)),
+            dma((2 * count,)),
             dma((count,)),
             dma((count // 2, 2)),
             pltpu.SemaphoreType.REGULAR,

time: 144 us -> 142 us (0.986)
  Pallas kernels: 142 us -> 140 us
    pallas_call x1, Pallas kernels: 142 us -> 140 us  [shards(): pl.pallas_call(functools.partial(kernel, count, cells), out_shape=(vmem((...]
where the time goes in v4:
time: 142 us
  Pallas kernels  140 us (99%)
  local copies, waits for them, and re-layouts  1.6 us (1%)
    pallas_call x1, Pallas kernels, shards(): pl.pallas_call(functools.partial(kernel, count, cells), out_shape=(vmem((...  140 us

profile of v4, /device:TPU:69, one launch (start us, length us, event | category | flops | bytes accessed | tf_op | source)
XLA Modules:
  0.0 141.8 jit_solution(3770233221211949870)
XLA Ops:
  0.6 139.5 %paradiag.1 = (f32[2,256,512]{2,1,0:T(8,128)S(1)}, f32[2,128]{1,0:T(2,128)S(1)}) custom-call(f32[2,256,512]{2,1,0:T(8,128)} %it_hbm.1, f32[2,256,512]{2,1,0:T(8,128)} %fo_hbm.1, f32[256,512]{1,0:T(8,128)} %init_hbm.1, f32[256,512]{1,0:T(8,128)} %di_hbm.1, f32[112]{0:T(128)} %constant.2.clone.tab), custom_call_target="tpu_custom_call" | custom-call | tf_op jit(solution)/shard_map/paradiag/pallas_call | solution.py:891
  140.2 1.0 copy.8
  141.1 0.6 slice_reduce_fusion

commit v5 on v4

--- a/solution.py
+++ b/solution.py
@@ -486,7 +486,7 @@
     row_tiles = piece // 8
 
     def transform(p, carry):
-        r = pl.multiple_of((p // tiles) * 8, 8)
+        r = pl.multiple_of(lax.rem(p // tiles + c, row_tiles) * 8, 8)
         q = pl.multiple_of(lax.rem(p, tiles) * 128, 128)
         x = [by_cell[n, pl.ds(r, 8), pl.ds(q, 128)] for n in range(length)]
         f = rfft_list(x)
@@ -498,7 +498,7 @@
                 spec[(j // share, 2 * (j % share) + part) + here] = f[j][part]
         return carry
 
-    lax.fori_loop(0, row_tiles * tiles, transform, 0)
+    lax.fori_loop(0, tiles, transform, 0)
 
     beyond = {"tm": lax.rem(t + count + 2 * c - 1, count)}
     src_edge = pl.ds(pl.multiple_of(8 + (slab - 8) * c, 8), 8)
@@ -531,10 +531,15 @@
     def send_halo(q, carry):
         halo(0, q).start()
         halo(1, q).start()
+        return carry
+
+    def send_swap(q, carry):
         swap(q).start()
         return carry
 
     lax.fori_loop(0, share, send_halo, 0)
+    lax.fori_loop(tiles, row_tiles * tiles, transform, 0)
+    lax.fori_loop(0, share, send_swap, 0)
 
     top = jnp.where(t == 0, 0.0, 1.0)
     bottom = jnp.where(t == count - 1, 0.0, 1.0)
@@ -660,21 +665,24 @@
     ar_send[...] = mine
     ar_all[me] = mine
 
-    def tell(k):
+    def tell(k, dest, core):
         return pltpu.make_async_remote_copy(
             src_ref=ar_send,
             dst_ref=ar_all.at[me],
-            send_sem=m_send.at[k],
+            send_sem=m_send.at[2 * k + core],
             recv_sem=m_recv.at[me],
-            device_id=pos(lax.rem(me + k, total)),
+            device_id={"tm": dest, "rows": core},
             device_id_type=MESH,
         )
 
     def tell_one(k, carry):
-        tell(k).start()
-        return carry
-
-    lax.fori_loop(1, total, tell_one, 0)
+        dest = peer(k)
+        tell(k, dest, 0).start()
+        tell(k, dest, 1).start()
+        return carry
+
+    lax.fori_loop(0, count - 1, tell_one, 0)
+    tell(count - 1, t, 1 - c).start()
 
     def told(k, carry):
         source = lax.rem(me + k, total)
@@ -771,7 +779,8 @@
         jnp.sum(jnp.sum(sq_send[...] + sq_recv[...], axis=2, keepdims=True), axis=1, keepdims=True) / cells
         + rms_eps
     )
-    rms_ref[...] = jnp.broadcast_to(rms[:, 0], (2, 128))
+    for i in range(2):
+        rms_ref[i] = rms[i, 0, 0]
 
     def final(source, core, piece_of):
         start = block_of(source, core)
@@ -855,10 +864,13 @@
     lax.fori_loop(0, share, drain_pairs, 0)
 
     def drain_tell(k, carry):
-        tell(k).wait_send()
-        return carry
-
-    lax.fori_loop(1, total, drain_tell, 0)
+        dest = peer(k)
+        tell(k, dest, 0).wait_send()
+        tell(k, dest, 1).wait_send()
+        return carry
+
+    lax.fori_loop(0, count - 1, drain_tell, 0)
+    tell(count - 1, t, 1 - c).wait_send()
 
 
 def tables(length):
@@ -892,10 +904,10 @@
         functools.partial(kernel, count, cells),
         out_shape=(
             vmem((steps, rows, cols), f32),
-            vmem((steps, 128), f32),
+            jax.ShapeDtypeStruct((steps,), f32),
         ),
         in_specs=[hbm] * 4 + [pl.BlockSpec(memory_space=pltpu.SMEM)],
-        out_specs=(pl.BlockSpec(memory_space=vmem), pl.BlockSpec(memory_space=vmem)),
+        out_specs=(pl.BlockSpec(memory_space=vmem), pl.BlockSpec(memory_space=pltpu.SMEM)),
         scratch_shapes=[
             vmem((steps, rows + 16, cols), f32),
             vmem((steps, rows, cols), f32),
@@ -939,7 +951,7 @@
         compiler_params=pltpu.CompilerParams(collective_id=0, has_side_effects=True),
         name="paradiag",
     )(iterate, forcing, initial_state, diffusivity, jnp.asarray(tables(length)))
-    return updated, rms[:, 0]
+    return updated, rms
 
 
 def solution(mesh):

time: 142 us -> 141 us (level)
  no operation moved by 1% of the time
where the time goes in v5:
time: 141 us
  Pallas kernels  139 us (99%)
  local copies, waits for them, and re-layouts  1.49 us (1%)
    pallas_call x1, Pallas kernels, shards(): pl.pallas_call(functools.partial(kernel, count, cells), out_shape=(vmem((...  139 us

profile of v5, /device:TPU:69, one launch (start us, length us, event | category | flops | bytes accessed | tf_op | source)
XLA Modules:
  0.0 141.4 jit_solution(417518053149157864)
XLA Ops:
  0.6 139.2 %paradiag.1 = (f32[2,256,512]{2,1,0:T(8,128)S(1)}, f32[2]{0:T(128)}) custom-call(f32[2,256,512]{2,1,0:T(8,128)} %it_hbm.1, f32[2,256,512]{2,1,0:T(8,128)} %fo_hbm.1, f32[256,512]{1,0:T(8,128)} %init_hbm.1, f32[256,512]{1,0:T(8,128)} %di_hbm.1, f32[112]{0:T(128)} %constant.2.clone.tab), custom_call_target="tpu_custom_call" | custom-call | tf_op jit(solution)/shard_map/paradiag/pallas_call | solution.py:903
  139.9 0.0 copy-start
  139.9 1.0 copy.9
  140.8 0.0 copy-done
  140.8 0.5 copy.10
Async XLA Ops:
  139.9 1.0 copy-start
